TPU v7x, 512 devices: a whole 4x8x8 slice. The times are simulated.
512 devices in a mesh: gx: 8 (over z), gy: 8 (over y), gz: 8 (over x, core).
Axes of the slice: x: 4, y: 8, z: 8, core: 2. Of those that a mesh axis runs over, the one named last changes fastest.
Arguments:
- right_side: float32 [512, 512, 512], P('gx', 'gy', 'gz'), may hold values from -6 to 6
- guess: float32 [512, 512, 512], P('gx', 'gy', 'gz'), may hold values from -6 to 6
Outputs:
- solution: float32 [512, 512, 512], P('gx', 'gy', 'gz')
- residual: float32 [512, 512, 512], P('gx', 'gy', 'gz')
All inputs are finite; a program needn't handle non-finite values.
Results may differ from a plain program's by a relative error of at most 0.0003.
Values sent between devices are 32-bit elements.
No kernel may reach another device: no remote copies, remote signals or barrier semaphores. Data moves between devices by JAX's collectives and lax.ppermute only.
A program may use at most 256 MiB of HBM per device.

v0:
```python
import jax
import jax.numpy as jnp
from jax import lax
from jax.sharding import PartitionSpec as P

LEVELS = 7
COARSE_SWEEPS = 4


def padded_2(value, sides, width, wrap):
    for axis, dim in sides:
        count, length = lax.axis_size(axis), value.shape[dim]
        up = [(i, (i + 1) % count) for i in range(count if wrap else count - 1)]
        down = [(j, i) for i, j in up]
        last = lax.slice_in_dim(value, length - width, length, axis=dim)
        leading = lax.slice_in_dim(value, 0, width, axis=dim)
        before = lax.ppermute(last, axis, up)
        after = lax.ppermute(leading, axis, down)
        value = jnp.concatenate([before, value, after], axis=dim)
    return value


def face_total(padded):
    total = padded[2:, 1:-1, 1:-1] + padded[:-2, 1:-1, 1:-1]
    total = total + padded[1:-1, 2:, 1:-1] + padded[1:-1, :-2, 1:-1]
    total = total + padded[1:-1, 1:-1, 2:] + padded[1:-1, 1:-1, :-2]
    return total


def walls(index, total):
    return (index == 0).astype(jnp.float32) + (index == total - 1).astype(jnp.float32)


def frame(offsets, block, totals):
    first = (offsets[0] + lax.iota(jnp.int32, block[0]))[:, None, None]
    second = (offsets[1] + lax.iota(jnp.int32, block[1]))[None, :, None]
    third = (offsets[2] + lax.iota(jnp.int32, block[2]))[None, None, :]
    parity = (first + second + third) % 2
    diagonal = 6.0 + walls(first, totals[0]) + walls(second, totals[1]) + walls(third, totals[2])
    return (parity == 0, parity == 1, diagonal)


def level_frame(places, counts, size):
    offsets = tuple((place * size for place in places))
    totals = tuple((count * size for count in counts))
    return frame(offsets, (size, size, size), totals)


def relax(padded, source, colour, diagonal, scale):
    updated = (scale * source + face_total(padded)) / diagonal
    return jnp.where(colour, updated, padded[1:-1, 1:-1, 1:-1])


def residual_on(padded, source, diagonal, inverse):
    return source - (diagonal * padded[1:-1, 1:-1, 1:-1] - face_total(padded)) * inverse


def restrict(remainder):
    shape = remainder.shape
    grouped = remainder.reshape(shape[0] // 2, 2, shape[1] // 2, 2, shape[2] // 2, 2)
    return jnp.sum(grouped, axis=(1, 3, 5)) * 0.125


def odd_pad(field):
    for axis in range(3):
        count = field.shape[axis]
        lowest = -lax.slice_in_dim(field, 0, 1, axis=axis)
        highest = -lax.slice_in_dim(field, count - 1, count, axis=axis)
        field = jnp.concatenate([lowest, field, highest], axis=axis)
    return field


def prolong(padded):
    centre = padded[1:-1, 1:-1, 1:-1]
    below_first = 0.25 * (padded[:-2, 1:-1, 1:-1] - centre)
    above_first = 0.25 * (padded[2:, 1:-1, 1:-1] - centre)
    below_second = 0.25 * (padded[1:-1, :-2, 1:-1] - centre)
    above_second = 0.25 * (padded[1:-1, 2:, 1:-1] - centre)
    below_third = 0.25 * (padded[1:-1, 1:-1, :-2] - centre)
    above_third = 0.25 * (padded[1:-1, 1:-1, 2:] - centre)
    along_first = jnp.stack([below_first, above_first], axis=1)[:, :, :, None, :, None]
    along_second = jnp.stack([below_second, above_second], axis=2)[:, None, :, :, :, None]
    along_third = jnp.stack([below_third, above_third], axis=3)[:, None, :, None, :, :]
    fine = centre[:, None, :, None, :, None] + along_first + along_second + along_third
    shape = centre.shape
    return fine.reshape(2 * shape[0], 2 * shape[1], 2 * shape[2])


def down_halo(field):
    return padded_2(field, (("gx", 0), ("gy", 1), ("gz", 2)), 1, False)


def up_halo(field):
    return padded_2(field, (("gx", 0), ("gy", 1), ("gz", 2)), 1, False)


def lift_halo(field):
    return padded_2(field, (("gx", 0), ("gy", 1), ("gz", 2)), 1, False)


def pad_zero(field):
    return jnp.pad(field, 1)


def reflect(padded, axis, lowest, highest):
    moved = jnp.moveaxis(padded, axis, 0)
    moved = moved.at[0].set(jnp.where(lowest, -moved[1], moved[0]))
    moved = moved.at[-1].set(jnp.where(highest, -moved[-2], moved[-1]))
    return jnp.moveaxis(moved, 0, axis)


def reflect_all(padded, places, counts):
    for axis in range(3):
        padded = reflect(padded, axis, places[axis] == 0, places[axis] == counts[axis] - 1)
    return padded


def descend(field, source, level, geometry):
    red, black, diagonal = geometry
    scale = 4.0**level
    if level == 0:
        first = relax(down_halo(field), source, red, diagonal, scale)
    else:
        first = jnp.where(red, scale * source / diagonal, 0.0)
    second = relax(down_halo(first), source, black, diagonal, scale)
    remainder = residual_on(down_halo(second), source, diagonal, 0.25**level)
    return (second, restrict(remainder))


def ascend(smoothed, source, padded, level, geometry):
    red, black, diagonal = geometry
    scale = 4.0**level
    fine = smoothed + prolong(padded)
    first = relax(up_halo(fine), source, red, diagonal, scale)
    return relax(up_halo(first), source, black, diagonal, scale)


def bottom_sweeps(source, geometry, scale, widen):
    red, black, diagonal = geometry
    field = jnp.where(red, scale * source / diagonal, 0.0)
    field = relax(widen(field), source, black, diagonal, scale)
    for sweep_index in range(COARSE_SWEEPS - 1):
        field = relax(widen(field), source, red, diagonal, scale)
        field = relax(widen(field), source, black, diagonal, scale)
    return field


def collect(source, counts):
    block = source.shape
    whole = lax.all_gather(source.reshape(1, -1), ("gx", "gy", "gz"), axis=0, tiled=True)
    grid = whole.reshape(counts + block)
    grid = jnp.transpose(grid, (0, 3, 1, 4, 2, 5))
    return grid.reshape(counts[0] * block[0], counts[1] * block[1], counts[2] * block[2])


def bottom(source, places, counts):
    scale = 4.0 ** (LEVELS - 1)
    size = source.shape[0]
    whole = collect(source, counts)
    correction = bottom_sweeps(whole, frame((0, 0, 0), whole.shape, whole.shape), scale, pad_zero)
    starts = (places[0] * size, places[1] * size, places[2] * size)
    padded = lax.dynamic_slice(odd_pad(correction), starts, (size + 2, size + 2, size + 2))
    return padded


def per_device(right_side, guess):
    counts = (lax.axis_size("gx"), lax.axis_size("gy"), lax.axis_size("gz"))
    places = (lax.axis_index("gx"), lax.axis_index("gy"), lax.axis_index("gz"))
    block = right_side.shape[0]
    frames = [level_frame(places, counts, block >> level) for level in range(LEVELS - 1)]
    field = guess
    source = right_side
    sources = []
    kept = []
    for level in range(LEVELS - 1):
        smoothed, coarse = descend(field, source, level, frames[level])
        sources.append(source)
        kept.append(smoothed)
        field = coarse
        source = coarse
    padded = bottom(source, places, counts)
    fine = guess
    for level in reversed(range(LEVELS - 1)):
        fine = ascend(kept[level], sources[level], padded, level, frames[level])
        if level > 0:
            padded = reflect_all(lift_halo(fine), places, counts)
    red, black, diagonal = frames[0]
    return (fine, residual_on(up_halo(fine), right_side, diagonal, 1.0))


def solution(mesh):
    return jax.shard_map(
        per_device,
        mesh=mesh,
        in_specs=(P("gx", "gy", "gz"), P("gx", "gy", "gz")),
        out_specs=(P("gx", "gy", "gz"), P("gx", "gy", "gz")),
        check_vma=False,
    )
```

profile of v0, /device:TPU:1, one launch (start us, length us, event | category | flops | bytes accessed | tf_op | source)
XLA Modules:
  0.0 1409.0 jit_solution(637733215440395271)
XLA Ops:
  27.3 6.0 collective-permute-start.5
  43.2 11.7 fusion.1
  96.9 13.8 fusion.2
  157.2 15.9 %fusion.4 = f32[64,64,64]{2,1,0:T(8,128)} fusion(f32[64,64,64]{2,1,0:T(8,128)S(1)} %copy-done, f32[64,64,64]{2,1,0:T(8,128)} %copy-done.1, f32[66,66,1]{2,1,0:T(8,128)} %copy.290, f32[66,1,64]{2,1,0:T(1,128)S(1)} %collective-permute-done.14, f32[66,1,64]{2,1,0:T(1,128)S(1)} %collective-permute-done.15, f32[1,64,64]{2,1,0:T(8,128)S(1)} %collective-permute-done.12, ...), kind=kLoop, calls=%fused_computation.23 | loop fusion | flops 7077888 | bytes 3263776 | tf_op jit(solution)/shard_map/sub | solution.py:55
  173.2 71.5 %reshape.1848 = f32[32,2,32,2,32,2]{5,4,3,2,1,0:T(8,128)} reshape(f32[64,64,64]{2,1,0:T(8,128)} %fusion.4) | data formatting | bytes 2097152 | tf_op jit(solution)/shard_map/reshape | solution.py:60
  244.6 20.8 %reduce_sum.54 = f32[32,32,32]{2,1,0:T(8,128)S(1)} reduce(f32[32,2,32,2,32,2]{5,4,3,2,1,0:T(8,128)} %reshape.1848, f32[]{:T(128)} %constant.823.clone.1), dimensions={1,3,5}, to_apply=%region_0.1 | reduce | flops 229376 | bytes 1179652 | tf_op jit(solution)/shard_map/reduce_sum | solution.py:61
  339.9 7.1 reshape.1849
  395.1 7.4 collective-permute-start.41
  427.1 7.3 collective-permute-start.47
  454.2 7.3 collective-permute-start.53
  483.7 7.3 collective-permute-start.59
  510.1 7.2 collective-permute-start.65
  536.7 7.2 collective-permute-start.71
  561.9 7.1 collective-permute-start.77
  571.8 94.9 %all-reduce.7 = f32[512]{0:T(512)S(1)} all-reduce(f32[512]{0:T(512)S(1)} %dynamic-update-slice.90), channel_id=1, replica_groups=mesh['gx'=8,'gy'=8,'gz'=8] {'gx','gy','gz'}, use_global_device_ids=true, to_apply=%add.7 | all-reduce | flops 512 | bytes 4096
  749.7 6.5 collective-permute-start.94
  826.6 7.1 collective-permute-start.112
  887.5 6.4 collective-permute-start.125
  910.7 7.1 collective-permute-start.130
  978.1 7.3 collective-permute-start.143
  1003.3 7.3 collective-permute-start.148
  1031.2 6.4 broadcast_add_fusion.1
  1037.6 7.1 add.2485
  1099.2 5.8 collective-permute-start.161
  1128.2 6.6 collective-permute-start.166
  1149.3 7.2 scatter.149
  1160.5 9.3 copy.325
  1172.6 27.0 %broadcast_add_fusion = f32[32,2,32,2,32,2]{5,4,3,2,1,0:T(8,128)} fusion(f32[32,32,32,2]{3,2,1,0:T(8,128)} %copy.325, f32[32,2,32,2,32]{4,3,2,1,0:T(2,128)S(1)} %broadcast_add_fusion.2), kind=kLoop, calls=%fused_computation | loop fusion | flops 262144 | bytes 1835008 | tf_op jit(solution)/shard_map/add | solution.py:84
  1199.6 54.9 %add.2507 = f32[64,64,64]{2,1,0:T(8,128)} reshape(f32[32,2,32,2,32,2]{5,4,3,2,1,0:T(8,128)} %broadcast_add_fusion) | data formatting | bytes 2097152 | tf_op jit(solution)/shard_map/add | solution.py:84
  1292.5 13.8 fusion.5
  1342.0 13.8 fusion.6
  1392.0 16.4 %fusion.8 = f32[64,64,64]{2,1,0:T(8,128)} fusion(f32[64,64,64]{2,1,0:T(8,128)S(1)} %copy-done, f32[64,64,64]{2,1,0:T(8,128)} %copy-done.3, f32[66,66,1]{2,1,0:T(8,128)} %copy.337, f32[66,1,64]{2,1,0:T(1,128)S(1)} %collective-permute-done.182, f32[66,1,64]{2,1,0:T(1,128)S(1)} %collective-permute-done.183, f32[1,64,64]{2,1,0:T(8,128)S(1)} %collective-permute-done.180, ...), kind=kLoop, calls=%fused_computation.27 | loop fusion | flops 7077888 | bytes 3263776 | tf_op jit(solution)/shard_map/sub | solution.py:55
  (840 shorter events, 893.8 us)
Async XLA Ops:
  1.4 9.5 collective-permute-start
  27.3 13.6 collective-permute-start.5
  82.8 11.8 collective-permute-start.11
  143.1 11.8 collective-permute-start.17
  288.0 10.8 collective-permute-start.23
  324.7 11.1 collective-permute-start.29
  366.7 8.7 collective-permute-start.34
  393.2 11.0 collective-permute-start.40
  395.1 10.2 collective-permute-start.41
  425.2 9.7 collective-permute-start.46
  427.1 9.0 collective-permute-start.47
  452.3 9.7 collective-permute-start.52
  454.2 8.9 collective-permute-start.53
  481.8 9.2 collective-permute-start.58
  508.2 9.1 collective-permute-start.64
  534.8 9.1 collective-permute-start.70
  559.9 9.0 collective-permute-start.76
  697.1 8.6 collective-permute-start.82
  721.2 8.8 collective-permute-start.88
  749.7 8.8 collective-permute-start.94
  801.4 9.0 collective-permute-start.106
  826.6 9.0 collective-permute-start.112
  885.1 9.0 collective-permute-start.124
  910.7 9.1 collective-permute-start.130
  976.2 10.9 collective-permute-start.142
  978.1 10.1 collective-permute-start.143
  1003.3 10.1 collective-permute-start.148
  1095.5 9.5 collective-permute-start.160
  1128.2 8.9 collective-permute-start.166
  1278.6 9.2 collective-permute-start.172
  1327.4 9.9 collective-permute-start.178
  1376.9 10.5 collective-permute-start.184
  (209 other events, 4022.0 us)
where the time goes:
time: 1430 us; the launch traced here: 1410 us
  starting transfers between devices  523 us (37%)
  local copies, waits for them, and re-layouts  304 us (21%)
  waiting for transfers between devices  248 us (17%)
  other arithmetic  226 us (16%)
  blocking collectives  94.9 us (7%)
    ppermute x93, starting transfers between devices, padded_2(): before = lax.ppermute(last, axis, up)  367 us
    ppermute x93, waiting for transfers between devices, padded_2(): after = lax.ppermute(leading, axis, down)  231 us
    ppermute x93, starting transfers between devices, padded_2(): after = lax.ppermute(leading, axis, down)  156 us
    unnamed x1, blocking collectives  94.9 us
    reshape x5, local copies, waits for them, and re-layouts, restrict(): remainder.reshape(shape[0] // 2, 2, shape[1] // 2, 2, shape[2] // 2, 2)  81.6 us
    select_n x26, other arithmetic, relax(): return jnp.where(colour, updated, padded[1:-1, 1:-1, 1:-1])  81 us
    add x5, local copies, waits for them, and re-layouts, prolong(): centre[:, None, :, None, :, None] + along_first + along_second + along_third  65.3 us
    slice x38, local copies, waits for them, and re-layouts, padded_2(): leading = lax.slice_in_dim(value, 0, width, axis=dim)  49.4 us
  transfers between devices with their start and end apart: 186, of which 96 were waited for; matrix products, arithmetic and copies ran while one was open for 3% of the time, Pallas kernels for 0%

commit v1 on v0

v1 whole, which is shorter than its diff:
```python
import functools
import typing

import jax
import jax.numpy as jnp
from jax import lax
from jax.experimental import pallas as pl
from jax.experimental.pallas import tpu as pltpu
from jax.sharding import PartitionSpec as P

F32 = jnp.float32
BF16 = jnp.bfloat16
COARSE_SWEEPS = 4
COUNT = 8


class Level(typing.NamedTuple):
    level: int
    pairs: int
    rows: int
    first: int
    offset: int
    size: int

    @property
    def scale(self):
        return 4.0**self.level

    @property
    def inverse(self):
        return 0.25**self.level

    @property
    def own(self):
        return self.size // 2

    def shape(self):
        return (self.pairs + 2, self.rows, 128)


L0 = Level(0, 40, 80, 3, 8, 64)
L1 = Level(1, 30, 64, 7, 16, 32)
L2 = Level(2, 14, 32, 3, 8, 16)
L3_OWN = Level(3, 6, 16, 1, 4, 8)
L3 = Level(3, 12, 24, 4, 8, 8)
L4 = Level(4, 16, 64, 0, 0, 32)
L5 = Level(5, 8, 32, 0, 0, 16)
L6 = Level(6, 4, 16, 0, 0, 8)


class Edges(typing.NamedTuple):
    ilo: typing.Any
    ihi: typing.Any
    jlo: typing.Any
    jhi: typing.Any
    klo: typing.Any
    khi: typing.Any


def block_edges():
    ends = []
    for axis in ("gx", "gy", "gz"):
        place = lax.axis_index(axis)
        ends += [place == 0, place == COUNT - 1]
    return Edges(*ends)


def whole_edges():
    yes = lax.axis_index("gx") >= 0
    return Edges(*([yes] * 6))


def lanes_of(shape):
    return lax.broadcasted_iota(jnp.int32, shape, len(shape) - 1)


def rows_of(shape):
    return lax.broadcasted_iota(jnp.int32, shape, len(shape) - 2)


def signed(lane):
    return jnp.where(lane < 96, lane, lane - 128)


def even_mask(rows):
    shape = (rows, 128)
    return ((rows_of(shape) + lanes_of(shape)) & 1) == 0


def turn(value, shift, axis):
    size = value.shape[axis]
    if isinstance(shift, int):
        shift %= size
        if shift == 0:
            return value
    return pltpu.roll(value, shift, axis)


def bounds(low, high, size):
    return jnp.where(low, 0, -4096), jnp.where(high, size, 4096)


def set_coefficients(lv, edges, c_ref, d_ref):
    shape = (lv.rows, 128)
    row = rows_of(shape) - lv.offset
    lane = signed(lanes_of(shape))
    row_low, row_high = bounds(edges.jlo, edges.jhi, lv.size)
    lane_low, lane_high = bounds(edges.klo, edges.khi, lv.size)
    inside = (row >= row_low) & (row < row_high) & (lane >= lane_low) & (lane < lane_high)
    diagonal = 6.0 + jnp.where(row == row_low, 1.0, 0.0) + jnp.where(row == row_high - 1, 1.0, 0.0)
    diagonal = diagonal + jnp.where(lane == lane_low, 1.0, 0.0) + jnp.where(lane == lane_high - 1, 1.0, 0.0)
    even = jnp.where(even_mask(lv.rows), 1.0, 0.0)
    for index, extra in enumerate((0.0, even, 1.0 - even)):
        d_ref[index] = diagonal + extra
        c_ref[index] = jnp.where(inside, 1.0 / (diagonal + extra), 0.0)
    c_ref[3] = jnp.zeros(shape, F32)


def kind(lv, edges, p, red):
    last = lv.first + lv.own - 1
    low, high = (1, 2) if red else (2, 1)
    inner = jnp.where((p == lv.first) & edges.ilo, low, jnp.where((p == last) & edges.ihi, high, 0))
    return jnp.where(((p < lv.first) & edges.ilo) | ((p > last) & edges.ihi), 3, inner)


def loop(low, high, body, unroll=1):
    def step(p, carry):
        body(p)
        return carry

    lax.fori_loop(low, high, step, 0, unroll=unroll)


def around(ref, p, even, red):
    value = ref[p + 1]
    before, after = ref[p], ref[p + 2]
    rows = value.shape[0]
    total = value + (jnp.where(even, before, after) if red else jnp.where(even, after, before))
    total = total + (turn(value, 1, 0) + turn(value, rows - 1, 0))
    return total + (turn(value, 1, 1) + turn(value, 127, 1))


def relax(lv, edges, c_ref, other, source, dest, low, high, red):
    even = even_mask(lv.rows)

    def body(p):
        total = around(other, p, even, red)
        if source is not None:
            total = total + (source[p + 1] if lv.level == 0 else lv.scale * source[p + 1])
        dest[p + 1] = total * c_ref[kind(lv, edges, p, red)]

    loop(low, high, body)


def relax_zero(lv, edges, c_ref, source, dest, low, high):
    loop(low, high, lambda p: dest.__setitem__(p + 1, lv.scale * source[p + 1] * c_ref[kind(lv, edges, p, True)]))


def remainder_at(lv, edges, d_ref, g_red, g_black, red, black, p, even):
    def one(mine, theirs, source, is_red):
        d = d_ref[jnp.minimum(kind(lv, edges, p, is_red), 2)]
        gap = d * mine[p + 1] - around(theirs, p, even, is_red)
        return source[p + 1] - (gap if lv.level == 0 else lv.inverse * gap)

    return one(red, black, g_red, True), one(black, red, g_black, False)


def clear_guards(lv, *refs):
    for ref in refs:
        ref[0] = jnp.zeros(ref.shape[1:], F32)
        ref[ref.shape[0] - 1] = jnp.zeros(ref.shape[1:], F32)


def split_dot(value, weights):
    high = value.astype(BF16)
    low = (value - high.astype(F32)).astype(BF16)
    return jnp.dot(jnp.concatenate([high, low], axis=1), weights, preferred_element_type=F32)


def halving_weights(own_lanes):
    shape = (256, 128)
    fine = signed(rows_of(shape) & 127)
    coarse = signed(lanes_of(shape))
    hit = (fine >> 1) == coarse
    if own_lanes:
        hit = hit & (fine >= 0) & (fine < own_lanes)
    return jnp.where(hit, 0.125, 0.0).astype(BF16)


def doubling_weights(size, low, high):
    shape = (256, 256)
    coarse = signed(rows_of(shape) & 127)
    lane = lanes_of(shape)
    fine = signed(lane & 127)
    parent = fine >> 1
    beside = parent + jnp.where((fine & 1) == 1, 1, -1)
    beyond = ((beside == -1) & low) | ((beside == size) & high)
    centre = jnp.where(coarse == parent, 0.25, 0.0)
    neighbour = jnp.where(coarse == beside, 0.25, 0.0)
    mixed = jnp.where(beyond, 0.0, centre + neighbour)
    return jnp.where(lane < 128, mixed, centre).astype(BF16)


def restrict(lv, edges, d_ref, g_red, g_black, red, black, low, count, row_low, rows, y_ref, z_ref, out_ref, own_lanes):
    even = even_mask(lv.rows)
    half = rows // 2

    def body(t):
        r_red, r_black = remainder_at(lv, edges, d_ref, g_red, g_black, red, black, low + t, even)
        y_ref[t] = r_red + r_black

    loop(0, count, body)

    def fold(t):
        z_ref[t] = y_ref[t, pl.ds(row_low, half, stride=2), :] + y_ref[t, pl.ds(row_low + 1, half, stride=2), :]

    loop(0, count, fold)
    weights = halving_weights(own_lanes)
    chunk = max(c for c in range(1, count + 1) if count % c == 0 and (c * half <= 256 or c == 1))

    def product(n):
        value = z_ref[pl.ds(n * chunk, chunk)].reshape(chunk * half, 128)
        out_ref[pl.ds(n * chunk, chunk)] = split_dot(value, weights).reshape(chunk, half, 128)

    loop(0, count // chunk, product)


def colour_planes(planes, pairs, red, black):
    even = even_mask(planes.shape[1])

    def body(p):
        low, high = planes[2 * p], planes[2 * p + 1]
        red[p + 1] = jnp.where(even, low, high)
        black[p + 1] = jnp.where(even, high, low)

    loop(0, pairs, body)


def whole_planes(red, black, pair_low, pairs, row_low, rows, e_ref, start=0):
    even = even_mask(rows)

    def body(t):
        r = red[pair_low + t + 1, pl.ds(row_low, rows), :]
        b = black[pair_low + t + 1, pl.ds(row_low, rows), :]
        e_ref[start + 2 * t] = jnp.where(even, r, b)
        e_ref[start + 2 * t + 1] = jnp.where(even, b, r)

    loop(0, pairs, body)


def prolong(e_ref, count, rows, row_zero, plane_zero, size, edges, near, plain):
    weights = doubling_weights(size, edges.klo, edges.khi)
    chunk = max(c for c in range(1, count + 1) if count % c == 0 and (c * rows <= 320 or c == 1))
    shape = (rows, 128)
    row = rows_of(shape) - row_zero
    at_low = (row == 0) & edges.jlo
    at_high = (row == size - 1) & edges.jhi

    def body(n):
        both = split_dot(e_ref[pl.ds(n * chunk, chunk)].reshape(chunk * rows, 128), weights).reshape(chunk, rows, 256)
        for c in range(chunk):
            t = n * chunk + c
            mixed, value = both[c, :, :128], both[c, :, 128:]
            before = jnp.where(at_low, -value, turn(value, 1, 0))
            after = jnp.where(at_high, -value, turn(value, rows - 1, 0))
            near[t, pl.ds(0, rows, stride=2), :] = mixed + before
            near[t, pl.ds(1, rows, stride=2), :] = mixed + after
            plain[t, pl.ds(0, rows, stride=2), :] = value
            plain[t, pl.ds(1, rows, stride=2), :] = value

    loop(0, count // chunk, body)
    if plane_zero > 0:
        pl.when(edges.ilo)(lambda: plain.__setitem__(plane_zero - 1, -plain[plane_zero]))
    last = plane_zero + size - 1
    if last + 1 < count:
        pl.when(edges.ihi)(lambda: plain.__setitem__(last + 1, -plain[last]))


def correct(lv, edges, c_ref, kept, near, plain, plane_zero, dest, low, high):
    even = even_mask(lv.rows)

    def body(p):
        t = p - lv.first + plane_zero
        step = near[t, : lv.rows] + jnp.where(even, plain[t + 1, : lv.rows], plain[t - 1, : lv.rows])
        c = c_ref[kind(lv, edges, p, False)]
        dest[p + 1] = jnp.where(c > 0.0, kept[p + 1] + step, 0.0)

    loop(low, high, body)


def compact_kernel(guess, source, x_ref, y_ref):
    even = ((rows_of((64, 64)) + lanes_of((64, 64))) & 1) == 0

    def body(u):
        blacks = []
        for s in range(2):
            p = 2 * u + s
            low, high = guess[2 * p], guess[2 * p + 1]
            f_low, f_high = source[2 * p], source[2 * p + 1]
            x_ref[p] = jnp.concatenate([jnp.where(even, high, low), jnp.where(even, f_low, f_high)], axis=1)
            blacks.append(jnp.where(even, f_high, f_low))
        y_ref[u] = jnp.concatenate(blacks, axis=1)

    loop(0, 16, body)


def pack_kernel(ib, ia, x, y, jb, ja, xf, yf, ku, kd):
    zero = jnp.zeros((80, 128), F32)
    for p in range(3):
        xf[p, 8:72] = ib[p]
        xf[35 + p, 8:72] = ia[p]
    loop(0, 32, lambda p: xf.__setitem__((p + 3, slice(8, 72)), x[p]))
    yf[0, 8:72] = ib[3]
    yf[17, 8:72] = ia[3]
    loop(0, 16, lambda p: yf.__setitem__((p + 1, slice(8, 72)), y[p]))

    def ends(p):
        xf[p, 0:8] = jb[p]
        xf[p, 72:80] = ja[p]

    loop(0, 38, ends)

    def more(p):
        yf[p, 0:8] = jb[p + 38]
        yf[p, 72:80] = ja[p + 38]

    loop(0, 18, more)
    for p in (38, 39):
        xf[p] = zero
    for p in range(18, 24):
        yf[p] = zero
    half = lanes_of((80, 128)) & 63
    lane = lanes_of((80, 128))
    x_down = (lane < 5) | ((lane >= 64) & (lane < 68))
    x_up = ((lane >= 59) & (lane < 64)) | (lane >= 124)
    y_down = half < 3
    y_up = half >= 61
    for u in range(5):
        down, up = zero, zero
        for s in range(8):
            value = xf[8 * u + s]
            down = down + turn(jnp.where(x_down, value, 0.0), 8 * s, 1)
            up = up + turn(jnp.where(x_up, value, 0.0), 8 * s, 1)
            if u < 3:
                value = yf[8 * u + s]
                down = down + turn(jnp.where(y_down, value, 0.0), 8 * s + 5, 1)
                up = up + turn(jnp.where(y_up, value, 0.0), 8 * s + 3, 1)
        kd[u] = down
        ku[u] = up


def fine_kernel(xf, yf, kb, ka, v_black, g_red, g_black, low_quads, high_quads, black, red, y_ref, z_ref, planes, c_ref, d_ref):
    edges = block_edges()
    set_coefficients(L0, edges, c_ref, d_ref)
    zero = jnp.zeros((80, 128), F32)
    lane = lanes_of((80, 128))
    own = lane < 64
    for u in range(5):
        below, above = kb[u], ka[u]
        for s in range(8):
            p = 8 * u + s
            value = xf[p]
            place = (lane - 8 * s) & 127
            edge = jnp.where(place < 5, above, jnp.where((place >= 59) & (place < 64), below, 0.0))
            black[p + 1] = jnp.where(own, value, turn(edge, 64 - 8 * s, 1))
            edge = jnp.where((place >= 64) & (place < 68), above, jnp.where(place >= 124, below, 0.0))
            g_red[p + 1] = jnp.where(own, turn(value, 64, 1), turn(edge, -8 * s, 1))
            if 8 * u + s < 18:
                value = yf[p]
                high = turn(above, 59 - 8 * s, 1)
                low = turn(below, 61 - 8 * s, 1)
                edge = jnp.where((lane >= 64) & (lane < 67), high, jnp.where(lane >= 125, low, 0.0))
                g_black[2 * p + 2] = jnp.where(own, value, edge)
                high, low, value = turn(high, 64, 1), turn(low, 64, 1), turn(value, 64, 1)
                edge = jnp.where((lane >= 64) & (lane < 67), high, jnp.where(lane >= 125, low, 0.0))
                g_black[2 * p + 3] = jnp.where(own, value, edge)
    for q in (0, 1, 38, 39, 40, 41):
        g_black[q] = zero
    clear_guards(L0, black, g_red, red, v_black)
    for q in (1, 38, 39, 40):
        red[q] = zero
        v_black[q] = zero
    relax(L0, edges, c_ref, black, g_red, red, 1, 37, True)
    relax(L0, edges, c_ref, red, g_black, v_black, 1, 37, False)
    restrict(L0, edges, d_ref, g_red, g_black, red, v_black, 3, 32, 8, 64, y_ref, z_ref, planes, 64)

    def quad(q, out):
        total = planes[4 * q]
        for m in range(1, 4):
            total = total + turn(planes[4 * q + m], 32 * m, 1)
        return total

    for q in range(4):
        low_quads[q] = quad(q, None)
        high_quads[q] = quad(q + 4, None)


def pack_quads_kernel(ib, ia, low_quads, high_quads, jb, ja, qf, ku, kd):
    for index, part in enumerate((ib, low_quads, high_quads, ia)):
        for q in range(4):
            qf[4 * index + q, 16:48] = part[q]
    for q in range(16):
        qf[q, 0:16] = jb[q]
        qf[q, 48:64] = ja[q]
    low_half = (lanes_of((64, 128)) & 31) < 16
    for u in range(8):
        first, second = qf[2 * u], qf[2 * u + 1]
        kd[u] = jnp.where(low_half, first, turn(second, 16, 1))
        ku[u] = jnp.where(low_half, turn(first, -16, 1), second)


def middle_kernel(
    qf, kb, ka, v1, gr1, gb1, v2, gr2, gb2, message,
    red1, y1, z1, p1, red2, y2, z2, p2, gr3, gb3, red3, black3, y3, z3, p3,
    c1, d1, c2, d2, c3, d3,
):
    edges = block_edges()
    for lv, c, d in ((L1, c1, d1), (L2, c2, d2), (L3_OWN, c3, d3)):
        set_coefficients(lv, edges, c, d)
    lane = lanes_of((64, 128))
    even = even_mask(64)

    def unpack(u):
        below, above = kb[u], ka[u]
        for h in range(2):
            value = qf[2 * u + h]
            for t in range(2):
                pair = []
                for m in (2 * t, 2 * t + 1):
                    at = 32 * m + 16 * h
                    right = turn(above, 32 - at, 1)
                    left = turn(below, 112 - at, 1)
                    edge = jnp.where(lane < 48, right, jnp.where(lane >= 112, left, 0.0))
                    pair.append(jnp.where(lane < 32, turn(value, -32 * m, 1), edge))
                index = 4 * u + 2 * h + t
                gr1[index] = jnp.where(even, pair[0], pair[1])
                gb1[index] = jnp.where(even, pair[1], pair[0])

    loop(0, 8, unpack)
    clear_guards(L1, red1, v1)
    relax_zero(L1, edges, c1, gr1, red1, 0, 30)
    relax(L1, edges, c1, red1, gb1, v1, 0, 30, False)
    restrict(L1, edges, d1, gr1, gb1, red1, v1, 1, 28, 0, 64, y1, z1, p1, 0)
    colour_planes(p1, 14, gr2, gb2)
    clear_guards(L2, red2, v2, gr2, gb2)
    relax_zero(L2, edges, c2, gr2, red2, 0, 14)
    relax(L2, edges, c2, red2, gb2, v2, 0, 14, False)
    restrict(L2, edges, d2, gr2, gb2, red2, v2, 1, 12, 0, 32, y2, z2, p2, 0)
    colour_planes(p2, 6, gr3, gb3)
    clear_guards(L3_OWN, red3, black3)
    relax_zero(L3_OWN, edges, c3, gr3, red3, 0, 6)
    relax(L3_OWN, edges, c3, red3, gb3, black3, 0, 6, False)
    restrict(L3_OWN, edges, d3, gr3, gb3, red3, black3, 1, 4, 0, 16, y3, z3, p3, 8)
    lane = lanes_of((8, 128))
    row = rows_of((8, 128))
    third = jnp.zeros((8, 128), F32)
    for i in range(8):
        third = third + turn(jnp.where(lane < 8, p2[i + 2, 4:12], 0.0), 8 * i, 1)
    fourth = jnp.zeros((8, 128), F32)
    for i in range(4):
        fourth = fourth + turn(jnp.where((lane < 4) & (row >= 2) & (row < 6), p3[i], 0.0), 32 * i, 1)
    fourth = pltpu.roll(fourth, 4 * lax.axis_index("gz"), 1)
    fourth = jnp.where((lax.axis_index("gy") & 1) == 0, turn(fourth, 6, 0), turn(fourth, 2, 0))

    def store(n):
        message[n, 0] = third
        message[n, 1] = fourth

    loop(0, 64, store)


def plane_kernel(tiles, message):
    y, z = lax.axis_index("gy"), lax.axis_index("gz")
    parts = []
    for t in range(4):
        total = tiles[16 * t, 1]
        for n in range(1, 16):
            total = total + tiles[16 * t + n, 1]
        parts.append(total)
    window = []
    for dy in range(3):
        for dz in range(3):
            yy, zz = y + (dy - 1), z + (dz - 1)
            inside = (yy >= 0) & (yy < COUNT) & (zz >= 0) & (zz < COUNT)
            index = jnp.clip(yy, 0, COUNT - 1) * COUNT + jnp.clip(zz, 0, COUNT - 1)
            window.append(jnp.where(inside, tiles[index, 0], 0.0))
    window.append(jnp.zeros((8, 128), F32))
    for n in range(5):
        parts.append(window[2 * n] + turn(window[2 * n + 1], 64, 1))

    def store(n):
        for index, part in enumerate(parts):
            message[n, index] = part

    loop(0, 8, store)


def coarse_kernel(
    tiles, v2, gr2, gb2, v1, gr1, gb1, v0, gr0, gb0, out, rest,
    gr4, gb4, red4, v4, y4, z4, p4, gr5, gb5, red5, v5, y5, z5, p5, gr6, gb6, red6, v6, full, window,
    gr3, gb3, red3, v3, b3, b2, red2, b1, red1, b0, red0, e_ref, near, plain,
    c0, d0, c1, d1, c2, d2, c3, d3, c4, d4, c5, d5, c6, d6,
):
    edges = block_edges()
    whole = whole_edges()
    for lv, c, d in ((L0, c0, d0), (L1, c1, d1), (L2, c2, d2), (L3, c3, d3)):
        set_coefficients(lv, edges, c, d)
    for lv, c, d in ((L4, c4, d4), (L5, c5, d5), (L6, c6, d6)):
        set_coefficients(lv, whole, c, d)
    x, y, z = (lax.axis_index(axis) for axis in ("gx", "gy", "gz"))

    lane = signed(lanes_of((8, 128)))
    even8 = even_mask(8)
    for dx in range(3):
        at = x + (dx - 1)
        inside = (at >= 0) & (at < COUNT)
        at = jnp.clip(at, 0, COUNT - 1)
        for dy in range(3):
            parts = [jnp.where(inside, tiles[at, 4 + (3 * dy + dz) // 2], 0.0) for dz in range(3)]
            for pair in range(4):
                both = []
                for i in (2 * pair, 2 * pair + 1):
                    total = jnp.zeros((8, 128), F32)
                    for dz in range(3):
                        shift = 8 * (dz - 1) - 8 * i - 64 * ((3 * dy + dz) % 2)
                        hit = (lane >= 8 * (dz - 1)) & (lane < 8 * dz)
                        total = jnp.where(hit, turn(parts[dz], shift, 1), total)
                    both.append(total)
                index = 4 * dx + pair + 1
                gr3[index, 8 * dy : 8 * dy + 8] = jnp.where(even8, both[0], both[1])
                gb3[index, 8 * dy : 8 * dy + 8] = jnp.where(even8, both[1], both[0])
    clear_guards(L3, red3, v3)
    relax_zero(L3, edges, c3, gr3, red3, 0, 12)
    relax(L3, edges, c3, red3, gb3, v3, 0, 12, False)

    lane = lanes_of((32, 128))
    even32 = even_mask(32)
    zero = jnp.zeros((32, 128), F32)

    def place(n):
        value = tiles[n, 0:4].reshape(32, 128)
        for t in range(2):
            low = jnp.where(lane < 32, turn(value, -64 * t, 1), 0.0)
            high = jnp.where(lane < 32, turn(value, -64 * t - 32, 1), 0.0)
            index = 2 * n + t + 1
            gr4[index, 0:32] = jnp.where(even32, low, high)
            gb4[index, 0:32] = jnp.where(even32, high, low)
            gr4[index, 32:64] = zero
            gb4[index, 32:64] = zero

    loop(0, 8, place)
    clear_guards(L4, red4, v4, gr4, gb4)
    relax_zero(L4, whole, c4, gr4, red4, 0, 16)
    relax(L4, whole, c4, red4, gb4, v4, 0, 16, False)
    restrict(L4, whole, d4, gr4, gb4, red4, v4, 0, 16, 0, 64, y4, z4, p4, 32)
    colour_planes(p4, 8, gr5, gb5)
    clear_guards(L5, red5, v5, gr5, gb5)
    relax_zero(L5, whole, c5, gr5, red5, 0, 8)
    relax(L5, whole, c5, red5, gb5, v5, 0, 8, False)
    restrict(L5, whole, d5, gr5, gb5, red5, v5, 0, 8, 0, 32, y5, z5, p5, 16)
    colour_planes(p5, 4, gr6, gb6)
    clear_guards(L6, red6, v6)
    relax_zero(L6, whole, c6, gr6, red6, 0, 4)
    relax(L6, whole, c6, red6, gb6, v6, 0, 4, False)
    for sweep_index in range(COARSE_SWEEPS - 1):
        relax(L6, whole, c6, v6, gr6, red6, 0, 4, True)
        relax(L6, whole, c6, red6, gb6, v6, 0, 4, False)

    def lift(coarse_red, coarse_black, pair_low, pairs, row_low, rows, plane_zero, row_zero, size, at, fine, c, kept, dest, low, high):
        e = e_ref.at[0 : 2 * pairs + 2, 0:rows]
        n = near.at[0 : 2 * pairs + 2, 0 : 2 * rows]
        p = plain.at[0 : 2 * pairs + 2, 0 : 2 * rows]
        whole_planes(coarse_red, coarse_black, pair_low, pairs, row_low, rows, e)
        prolong(e, 2 * pairs, rows, row_zero, plane_zero, size, at, n, p)
        correct(fine, at, c, kept, n, p, plane_zero, dest, low, high)

    def smooth(lv, at, c, black, g_red, g_black, red, dest, low, high, low2, high2):
        relax(lv, at, c, black, g_red, red, low, high, True)
        relax(lv, at, c, red, g_black, dest, low2, high2, False)

    ascend_whole(L6, L5, whole, c5, red6, v6, v5, gr5, gb5, red5, y5, e_ref, near, plain)
    ascend_whole(L5, L4, whole, c4, red5, v5, v4, gr4, gb4, red4, y4, e_ref, near, plain)

    full[...] = jnp.zeros(full.shape, F32)
    even = even_mask(32)

    def spread(t):
        r, b = red4[t + 1, 0:32], v4[t + 1, 0:32]
        full[2 * t + 4, 8:40] = jnp.where(even, r, b)
        full[2 * t + 5, 8:40] = jnp.where(even, b, r)

    loop(0, 16, spread)

    def cut(t):
        rows = full[4 * x + t, pl.ds(4 * y + 4, 16), :]
        e_ref[t, 0:16] = pltpu.roll(rows, (128 - 4 * z) & 127, 1)

    loop(0, 12, cut)
    n, p = near.at[0:12, 0:32], plain.at[0:12, 0:32]
    prolong(e_ref.at[0:12, 0:16], 12, 16, 4, 4, 4, edges, n, p)
    correct(L3, edges, c3, v3, n, p, 4, b3, 1, 11)
    clear_guards(L3, b3, red3)
    smooth(L3, edges, c3, b3, gr3, gb3, red3, b3, 2, 10, 2, 10)

    lift(red3, b3, 2, 8, 4, 16, 4, 4, 8, edges, L2, c2, v2, b2, 0, 14)
    clear_guards(L2, b2, red2)
    smooth(L2, edges, c2, b2, gr2, gb2, red2, b2, 1, 13, 1, 13)

    lift(red2, b2, 1, 12, 0, 32, 4, 8, 16, edges, L1, c1, v1, b1, 5, 25)
    b1[5] = jnp.zeros(b1.shape[1:], F32)
    b1[26] = jnp.zeros(b1.shape[1:], F32)
    red1[6] = jnp.zeros(b1.shape[1:], F32)
    red1[25] = jnp.zeros(b1.shape[1:], F32)
    smooth(L1, edges, c1, b1, gr1, gb1, red1, b1, 5, 25, 6, 24)

    lift(red1, b1, 5, 20, 12, 40, 4, 4, 32, edges, L0, c0, v0, b0, 1, 37)
    b0[1] = jnp.zeros(b0.shape[1:], F32)
    b0[38] = jnp.zeros(b0.shape[1:], F32)
    smooth(L0, edges, c0, b0, gr0, gb0, red0, b0, 1, 37, 2, 36)

    even0 = even_mask(80)
    own = even_mask(64)[:, 0:64]

    def finish(t):
        p = t + 3
        r, b = red0[p + 1, 8:72, 0:64], b0[p + 1, 8:72, 0:64]
        out[2 * t] = jnp.where(own, r, b)
        out[2 * t + 1] = jnp.where(own, b, r)
        r, b = remainder_at(L0, edges, d0, gr0, gb0, red0, b0, p, even0)
        r, b = r[8:72, 0:64], b[8:72, 0:64]
        rest[2 * t] = jnp.where(own, r, b)
        rest[2 * t + 1] = jnp.where(own, b, r)

    loop(0, 32, finish)


def ascend_whole(coarse, fine, at, c, coarse_red, coarse_black, kept, g_red, g_black, red, scratch, e_ref, near, plain):
    rows = coarse.rows
    count = coarse.size
    e = e_ref.at[0:count, 0:rows]
    n = near.at[0 : count + 2, 0 : 2 * rows]
    p = plain.at[0 : count + 2, 0 : 2 * rows]
    whole_planes(coarse_red, coarse_black, 0, coarse.pairs, 0, rows, e)
    prolong(e, count, rows, 0, 0, count, at, near.at[1 : count + 1, 0 : 2 * rows], plain.at[1 : count + 1, 0 : 2 * rows])
    p[0] = -p[1]
    p[count + 1] = -p[count]
    correct(fine, at, c, kept, n, p, 1, kept, 0, fine.pairs)
    relax(fine, at, c, kept, g_red, red, 0, fine.pairs, True)
    relax(fine, at, c, red, g_black, kept, 0, fine.pairs, False)


def struct(*shape):
    return jax.ShapeDtypeStruct(shape, F32)


def call(kernel, outs, scratch, name, flops=2_000_000):
    space = pl.BlockSpec(memory_space=pltpu.VMEM)

    def run(*args):
        return pl.pallas_call(
            kernel,
            out_shape=outs,
            in_specs=[space] * len(args),
            out_specs=[space] * len(outs),
            scratch_shapes=[pltpu.VMEM(shape, F32) for shape in scratch],
            compiler_params=pltpu.CompilerParams(vmem_limit_bytes=40 * 2**20),
            cost_estimate=pl.CostEstimate(flops=flops, bytes_accessed=1_000_000, transcendentals=0),
            name=name,
        )(*args)

    return run


def pair(to_next, to_before, axis):
    up = [(i, i + 1) for i in range(COUNT - 1)]
    down = [(i + 1, i) for i in range(COUNT - 1)]
    return lax.ppermute(to_next, axis, up), lax.ppermute(to_before, axis, down)


def face(guess, source, start, first):
    even = ((lax.broadcasted_iota(jnp.int32, (64, 64), 0) + lax.broadcasted_iota(jnp.int32, (64, 64), 1)) & 1) == 0
    low, high = guess[start : start + 6 : 2], guess[start + 1 : start + 6 : 2]
    f_low, f_high = source[start : start + 6 : 2], source[start + 1 : start + 6 : 2]
    red = jnp.where(even, f_low, f_high)
    black = jnp.where(even, f_high, f_low)
    mixed = jnp.concatenate([jnp.where(even, high, low), red], axis=2)
    return jnp.concatenate([mixed, jnp.concatenate([black[first : first + 1], black[first + 1 : first + 2]], axis=2)], axis=0)


def coefficient_scratch(*levels):
    shapes = []
    for lv in levels:
        shapes += [(4, lv.rows, 128), (3, lv.rows, 128)]
    return shapes


def per_device(right_side, guess):
    ib, ia = pair(face(guess, right_side, 58, 1), face(guess, right_side, 0, 0), "gx")
    x, y = call(compact_kernel, (struct(32, 64, 128), struct(16, 64, 128)), [], "compact")(guess, right_side)

    def ends(low):
        parts = [ib[:3], x, ia[:3], ib[3:], y, ia[3:]]
        return jnp.concatenate([part[:, low : low + 8] for part in parts], axis=0)

    jb, ja = pair(ends(56), ends(0), "gy")
    xf, yf, ku, kd = call(
        pack_kernel, (struct(40, 80, 128), struct(24, 80, 128), struct(5, 80, 128), struct(5, 80, 128)), [], "pack"
    )(ib, ia, x, y, jb, ja)
    kb, ka = pair(ku, kd, "gz")
    fine = L0.shape()
    v0, gr0, gb0, low_quads, high_quads = call(
        fine_kernel,
        (struct(*fine), struct(*fine), struct(*fine), struct(4, 32, 128), struct(4, 32, 128)),
        [fine, fine, (32, 80, 128), (32, 32, 128), (32, 32, 128)] + coefficient_scratch(L0),
        "fine",
    )(xf, yf, kb, ka)

    ib, ia = pair(high_quads, low_quads, "gx")

    def quad_ends(low):
        return jnp.concatenate([part[:, low : low + 16] for part in (ib, low_quads, high_quads, ia)], axis=0)

    jb, ja = pair(quad_ends(16), quad_ends(0), "gy")
    qf, ku, kd = call(pack_quads_kernel, (struct(16, 64, 128), struct(8, 64, 128), struct(8, 64, 128)), [], "pack_quads")(
        ib, ia, low_quads, high_quads, jb, ja
    )
    kb, ka = pair(ku, kd, "gz")
    s1, s2, s3 = L1.shape(), L2.shape(), L3_OWN.shape()
    v1, gr1, gb1, v2, gr2, gb2, message = call(
        middle_kernel,
        tuple(struct(*s) for s in (s1, s1, s1, s2, s2, s2, (64, 2, 8, 128))),
        [s1, (28, 64, 128), (28, 32, 128), (28, 32, 128), s2, (12, 32, 128), (12, 16, 128), (12, 16, 128)]
        + [s3, s3, s3, s3, (4, 16, 128), (4, 8, 128), (4, 8, 128)]
        + coefficient_scratch(L1, L2, L3_OWN),
        "middle",
    )(qf, kb, ka)

    tiles = lax.all_to_all(message, ("gy", "gz"), 0, 0)
    (message,) = call(plane_kernel, (struct(8, 9, 8, 128),), [], "plane")(tiles)
    tiles = lax.all_to_all(message, "gx", 0, 0)
    s3, s4, s5, s6 = L3.shape(), L4.shape(), L5.shape(), L6.shape()
    return tuple(
        call(
            coarse_kernel,
            (struct(64, 64, 64), struct(64, 64, 64)),
            [s4, s4, s4, s4, (16, 64, 128), (16, 32, 128), (16, 32, 128)]
            + [s5, s5, s5, s5, (8, 32, 128), (8, 16, 128), (8, 16, 128)]
            + [s6, s6, s6, s6, (40, 48, 128), (12, 16, 128)]
            + [s3, s3, s3, s3, s3, s2, s2, s1, s1, fine, fine]
            + [(42, 40, 128), (42, 80, 128), (42, 80, 128)]
            + coefficient_scratch(L0, L1, L2, L3, L4, L5, L6),
            "coarse",
        )(tiles, v2, gr2, gb2, v1, gr1, gb1, v0, gr0, gb0)
    )


def solution(mesh):
    return jax.shard_map(
        per_device,
        mesh=mesh,
        in_specs=(P("gx", "gy", "gz"), P("gx", "gy", "gz")),
        out_specs=(P("gx", "gy", "gz"), P("gx", "gy", "gz")),
        check_vma=False,
    )
```

time: 1430 us -> 184 us (0.13); the launches traced: 1410 us -> 183 us
  starting transfers between devices: 523 us -> 37.5 us
  local copies, waits for them, and re-layouts: 304 us -> 1.67 us
  other arithmetic: 226 us -> 1.65 us
  waiting for transfers between devices: 248 us -> 25.6 us
  Pallas kernels: 0 us -> 69.8 us
  blocking collectives: 94.9 us -> 46.1 us
    ppermute x186 -> x12, starting transfers between devices: 523 us -> 37.5 us  [the longest x6 28.5 us: pair(): lax.ppermute(to_next, axis, up)]
    ppermute x186 -> x12, waiting for transfers between devices: 248 us -> 25.6 us  [the longest x6 21.5 us: pair(): lax.ppermute(to_before, axis, down)]
    unnamed x1 -> x0, blocking collectives: 94.9 us -> none
    select_n x52 -> x1, other arithmetic: 89.2 us -> 1.41 us  [face(): mixed = jnp.concatenate([jnp.where(even, high, low), red], axis=2)]
    reshape x5 -> x0, local copies, waits for them, and re-layouts: 81.6 us -> none  [restrict(): remainder.reshape(shape[0] // 2, 2, shape[1] // 2, 2, shape[2] // 2, 2)]
    slice x91 -> x5, local copies, waits for them, and re-layouts: 72.9 us -> 0.04 us  [the longest x3 0.02 us: quad_ends(): part[:, low:low + 16]]
    pallas_call x0 -> x7, Pallas kernels: none -> 69.8 us  [run(): pl.pallas_call(kernel, out_shape=outs, in_specs=[space] * len(args), out_...]
    add x5 -> x0, local copies, waits for them, and re-layouts: 65.3 us -> none  [prolong(): centre[:, None, :, None, :, None] + along_first + along_second + along_third]
  transfers between devices with their start and end apart: 186 -> 12, of which waited for: 96 -> 10; matrix products, arithmetic and copies ran while one was open for 3% -> 0% of each run, Pallas kernels for 0% -> 1%
where the time goes in v1:
time: 184 us; the launch traced here: 183 us
  Pallas kernels  69.8 us (38%)
  blocking collectives  46.1 us (25%)
  starting transfers between devices  37.5 us (20%)
  waiting for transfers between devices  25.6 us (14%)
    pallas_call x7, Pallas kernels, run(): pl.pallas_call(kernel, out_shape=outs, in_specs=[space] * len(args), out_...  69.8 us
    ppermute x6, starting transfers between devices, pair(): lax.ppermute(to_next, axis, up)  28.5 us
    all_to_all x1, blocking collectives, per_device(): tiles = lax.all_to_all(message, ('gy', 'gz'), 0, 0)  28.2 us
    ppermute x6, waiting for transfers between devices, pair(): lax.ppermute(to_before, axis, down)  21.5 us
    all_to_all x1, blocking collectives, per_device(): tiles = lax.all_to_all(message, 'gx', 0, 0)  17.8 us
    ppermute x6, starting transfers between devices, pair(): lax.ppermute(to_before, axis, down)  9.01 us
    ppermute x6, waiting for transfers between devices, pair(): lax.ppermute(to_next, axis, up)  4.14 us
  transfers between devices with their start and end apart: 12, of which 10 were waited for; matrix products, arithmetic and copies ran while one was open for 0% of the time, Pallas kernels for 1%

profile of v1, /device:TPU:1, one launch (start us, length us, event | category | flops | bytes accessed | tf_op | source)
XLA Modules:
  0.0 183.3 jit_solution(5354303405943222070)
XLA Ops:
  0.7 1.4 slice_select_fusion
  2.2 4.8 %collective-permute-start = (f32[4,64,128]{2,1,0:T(8,128)S(1)}, f32[4,64,128]{2,1,0:T(8,128)S(1)}, u32[]{:S(2)}, u32[]{:S(2)}) collective-permute-start(f32[4,64,128]{2,1,0:T(8,128)S(1)} %maximum_maximum_fusion), channel_id=1, source_target_pairs={{0,64},{64,128},{128,192},{192,256},{256,320},{320,384},{384,448},... | collective-permute-start | bytes 393224 | tf_op jit(solution)/shard_map/ppermute | solution.py:677
  7.2 1.3 collective-permute-start.1
  8.5 1.6 copy-done.1
  10.1 1.5 compact.1
  11.6 1.9 %collective-permute-done.1.ia = f32[4,64,128]{2,1,0:T(8,128)S(1)} collective-permute-done((f32[4,64,128]{2,1,0:T(8,128)S(1)}, f32[4,64,128]{2,1,0:T(8,128)S(1)}, u32[]{:S(2)}, u32[]{:S(2)}) %collective-permute-start.1) | collective-permute-done | bytes 131104 | tf_op jit(solution)/shard_map/ppermute | solution.py:677
  13.5 1.3 collective-permute-start.3
  14.8 4.4 %collective-permute-start.2 = (f32[56,8,128]{2,1,0:T(8,128)S(1)}, f32[56,8,128]{2,1,0:T(8,128)S(1)}, u32[]{:S(2)}, u32[]{:S(2)}) collective-permute-start(f32[56,8,128]{2,1,0:T(8,128)S(1)} %get-tuple-element.55), channel_id=1, source_target_pairs={{0,8},{8,16},{16,24},{24,32},{32,40},{40,48},{48,56},{1,9},{9,17},... | collective-permute-start | bytes 688136 | tf_op jit(solution)/shard_map/ppermute | solution.py:677
  19.3 1.5 collective-permute-done.3.ja
  20.7 1.5 collective-permute-done.2.jb
  22.2 1.9 %pack.1 = (f32[40,80,128]{2,1,0:T(8,128)S(1)}, f32[24,80,128]{2,1,0:T(8,128)S(1)}, f32[5,80,128]{2,1,0:T(8,128)S(1)}, f32[5,80,128]{2,1,0:T(8,128)S(1)}) custom-call(f32[4,64,128]{2,1,0:T(8,128)S(1)} %collective-permute-done.ib, f32[4,64,128]{2,1,0:T(8,128)S(1)} %collective-permute-done.1.ia, f32[32,64,128]{2,1,0:T(8,128)S(1)} %get-tuple-element.23.x, ...), custom_call_target="tpu_custom_call" | custom-call | flops 2000000 | bytes 1000000 | tf_op jit(solution)/shard_map/pack/pallas_call | solution.py:660
  24.1 6.0 %collective-permute-start.4 = (f32[5,80,128]{2,1,0:T(8,128)S(1)}, f32[5,80,128]{2,1,0:T(8,128)S(1)}, u32[]{:S(2)}, u32[]{:S(2)}) collective-permute-start(f32[5,80,128]{2,1,0:T(8,128)S(1)} %get-tuple-element.27), channel_id=1, source_target_pairs={{0,1},{1,2},{2,3},{3,4},{4,5},{5,6},{6,7},{8,9},{9,10},{10,11},{11... | collective-permute-start | bytes 614408 | tf_op jit(solution)/shard_map/ppermute | solution.py:677
  30.1 1.9 %collective-permute-start.5 = (f32[5,80,128]{2,1,0:T(8,128)S(1)}, f32[5,80,128]{2,1,0:T(8,128)S(1)}, u32[]{:S(2)}, u32[]{:S(2)}) collective-permute-start(f32[5,80,128]{2,1,0:T(8,128)S(1)} %get-tuple-element.28), channel_id=1, source_target_pairs={{1,0},{2,1},{3,2},{4,3},{5,4},{6,5},{7,6},{9,8},{10,9},{11,10},{12... | collective-permute-start | bytes 614408 | tf_op jit(solution)/shard_map/ppermute | solution.py:677
  32.0 0.7 collective-permute-done.4.kb
  32.8 4.4 %collective-permute-done.5.ka = f32[5,80,128]{2,1,0:T(8,128)S(1)} collective-permute-done((f32[5,80,128]{2,1,0:T(8,128)S(1)}, f32[5,80,128]{2,1,0:T(8,128)S(1)}, u32[]{:S(2)}, u32[]{:S(2)}) %collective-permute-start.5) | collective-permute-done | bytes 204832 | tf_op jit(solution)/shard_map/ppermute | solution.py:677
  37.2 14.7 %fine.1 = (f32[42,80,128]{2,1,0:T(8,128)S(1)}, f32[42,80,128]{2,1,0:T(8,128)S(1)}, f32[42,80,128]{2,1,0:T(8,128)S(1)}, f32[4,32,128]{2,1,0:T(8,128)S(1)}, f32[4,32,128]{2,1,0:T(8,128)S(1)}) custom-call(f32[40,80,128]{2,1,0:T(8,128)S(1)} %get-tuple-element.25.xf, f32[24,80,128]{2,1,0:T(8,128)S(1)} %get-tuple-element.26.yf, ...), custom_call_target="tpu_custom_call" | custom-call | flops 2000000 | bytes 1000000 | tf_op jit(solution)/shard_map/fine/pallas_call | solution.py:660
  51.9 4.0 %collective-permute-start.6 = (f32[4,32,128]{2,1,0:T(8,128)S(1)}, f32[4,32,128]{2,1,0:T(8,128)S(1)}, u32[]{:S(2)}, u32[]{:S(2)}) collective-permute-start(f32[4,32,128]{2,1,0:T(8,128)S(1)} %get-tuple-element.29.high_quads), channel_id=1, source_target_pairs={{0,64},{64,128},{128,192},{192,256},{256,320},{320,384},{384,448},... | collective-permute-start | bytes 196616 | tf_op jit(solution)/shard_map/ppermute | solution.py:677
  55.9 1.3 collective-permute-start.7
  57.2 5.5 %collective-permute-done.7.ia = f32[4,32,128]{2,1,0:T(8,128)S(1)} collective-permute-done((f32[4,32,128]{2,1,0:T(8,128)S(1)}, f32[4,32,128]{2,1,0:T(8,128)S(1)}, u32[]{:S(2)}, u32[]{:S(2)}) %collective-permute-start.7) | collective-permute-done | bytes 65568 | tf_op jit(solution)/shard_map/ppermute | solution.py:677
  62.8 4.1 %collective-permute-start.8 = (f32[16,16,128]{2,1,0:T(8,128)S(1)}, f32[16,16,128]{2,1,0:T(8,128)S(1)}, u32[]{:S(2)}, u32[]{:S(2)}) collective-permute-start(f32[16,16,128]{2,1,0:T(8,128)S(1)} %pad_maximum_fusion), channel_id=1, source_target_pairs={{0,8},{8,16},{16,24},{24,32},{32,40},{40,48},{48,56},{1,9},{9,17},... | collective-permute-start | bytes 393224 | tf_op jit(solution)/shard_map/ppermute | solution.py:677
  66.9 1.3 collective-permute-start.9
  68.2 0.6 collective-permute-done.8.jb
  68.8 3.8 %collective-permute-done.9.ja = f32[16,16,128]{2,1,0:T(8,128)S(1)} collective-permute-done((f32[16,16,128]{2,1,0:T(8,128)S(1)}, f32[16,16,128]{2,1,0:T(8,128)S(1)}, u32[]{:S(2)}, u32[]{:S(2)}) %collective-permute-start.9) | collective-permute-done | bytes 131104 | tf_op jit(solution)/shard_map/ppermute | solution.py:677
  72.6 0.2 pack_quads.1
  72.8 5.1 %collective-permute-start.10 = (f32[8,64,128]{2,1,0:T(8,128)S(1)}, f32[8,64,128]{2,1,0:T(8,128)S(1)}, u32[]{:S(2)}, u32[]{:S(2)}) collective-permute-start(f32[8,64,128]{2,1,0:T(8,128)S(1)} %get-tuple-element.32), channel_id=1, source_target_pairs={{0,1},{1,2},{2,3},{3,4},{4,5},{5,6},{6,7},{8,9},{9,10},{10,11},{11... | collective-permute-start | bytes 786440 | tf_op jit(solution)/shard_map/ppermute | solution.py:677
  78.0 1.9 %collective-permute-start.11 = (f32[8,64,128]{2,1,0:T(8,128)S(1)}, f32[8,64,128]{2,1,0:T(8,128)S(1)}, u32[]{:S(2)}, u32[]{:S(2)}) collective-permute-start(f32[8,64,128]{2,1,0:T(8,128)S(1)} %get-tuple-element.33), channel_id=1, source_target_pairs={{1,0},{2,1},{3,2},{4,3},{5,4},{6,5},{7,6},{9,8},{10,9},{11,10},{12... | collective-permute-start | bytes 786440 | tf_op jit(solution)/shard_map/ppermute | solution.py:677
  79.9 1.3 collective-permute-done.10.kb
  81.2 4.4 %collective-permute-done.11.ka = f32[8,64,128]{2,1,0:T(8,128)S(1)} collective-permute-done((f32[8,64,128]{2,1,0:T(8,128)S(1)}, f32[8,64,128]{2,1,0:T(8,128)S(1)}, u32[]{:S(2)}, u32[]{:S(2)}) %collective-permute-start.11) | collective-permute-done | bytes 262176 | tf_op jit(solution)/shard_map/ppermute | solution.py:677
  85.6 13.0 %middle.1 = (f32[32,64,128]{2,1,0:T(8,128)S(1)}, f32[32,64,128]{2,1,0:T(8,128)S(1)}, f32[32,64,128]{2,1,0:T(8,128)S(1)}, f32[16,32,128]{2,1,0:T(8,128)S(1)}, f32...) custom-call(f32[16,64,128]{2,1,0:T(8,128)S(1)} %get-tuple-element.31.qf, ...), custom_call_target="tpu_custom_call" | custom-call | flops 2000000 | bytes 1000000 | tf_op jit(solution)/shard_map/middle/pallas_call | solution.py:660
  98.7 28.2 %all_to_all.10.tiles = f32[64,2,8,128]{3,2,1,0:T(8,128)S(1)} all-to-all(f32[64,2,8,128]{3,2,1,0:T(8,128)S(1)} %get-tuple-element.34), channel_id=1, replica_groups=mesh['gx'=8,'gy'=8,'gz'=8] {'gy','gz'}, dimensions={0} | all-to-all | bytes 1048576 | tf_op jit(solution)/shard_map/all_to_all | solution.py:738
  127.0 17.8 %all_to_all.11.tiles = f32[8,9,8,128]{3,2,1,0:T(8,128)S(1)} all-to-all(f32[8,9,8,128]{3,2,1,0:T(8,128)S(1)} %plane.1), channel_id=1, replica_groups=mesh['gx'=8,'gy'=8,'gz'=8] {'gx'}, dimensions={0} | all-to-all | bytes 589824 | tf_op jit(solution)/shard_map/all_to_all | solution.py:740
  144.9 38.4 %coarse.1 = (f32[64,64,64]{2,1,0:T(8,128)}, f32[64,64,64]{2,1,0:T(8,128)}) custom-call(f32[8,9,8,128]{3,2,1,0:T(8,128)S(1)} %all_to_all.11.tiles, f32[16,32,128]{2,1,0:T(8,128)S(1)} %get-tuple-element.35.v2, f32[16,32,128]{2,1,0:T(8,128)S(1)} %get-tuple-element.36.gr2, f32[16,32,128]{2,1,0:T(8,128)S(1)} %get-tuple-element.37.gb2, ...), custom_call_target="tpu_custom_call" | custom-call | flops 2000000 | bytes 1000000 | tf_op jit(solution)/shard_map/coarse/pallas_call | solution.py:660
  (22 shorter events, 0.5 us)
Async XLA Ops:
  0.6 7.8 %copy-start = (f32[64,64,64]{2,1,0:T(8,128)S(1)}, f32[64,64,64]{2,1,0:T(8,128)}, u32[]{:S(2)}) copy-start(f32[64,64,64]{2,1,0:T(8,128)} %guess.1) | copy-start | bytes 3145732
  2.2 9.4 %collective-permute-start = (f32[4,64,128]{2,1,0:T(8,128)S(1)}, f32[4,64,128]{2,1,0:T(8,128)S(1)}, u32[]{:S(2)}, u32[]{:S(2)}) collective-permute-start(f32[4,64,128]{2,1,0:T(8,128)S(1)} %maximum_maximum_fusion), channel_id=1, source_target_pairs={{0,64},{64,128},{128,192},{192,256},{256,320},{320,384},{384,448},... | collective-permute-start | bytes 393224 | tf_op jit(solution)/shard_map/ppermute | solution.py:677
  7.2 6.3 %collective-permute-start.1 = (f32[4,64,128]{2,1,0:T(8,128)S(1)}, f32[4,64,128]{2,1,0:T(8,128)S(1)}, u32[]{:S(2)}, u32[]{:S(2)}) collective-permute-start(f32[4,64,128]{2,1,0:T(8,128)S(1)} %maximum_maximum_fusion.1), channel_id=1, source_target_pairs={{64,0},{128,64},{192,128},{256,192},{320,256},{384,320},{448,384},... | collective-permute-start | bytes 393224 | tf_op jit(solution)/shard_map/ppermute | solution.py:677
  8.5 1.6 copy-start.1
  13.5 7.2 %collective-permute-start.3 = (f32[56,8,128]{2,1,0:T(8,128)S(1)}, f32[56,8,128]{2,1,0:T(8,128)S(1)}, u32[]{:S(2)}, u32[]{:S(2)}) collective-permute-start(f32[56,8,128]{2,1,0:T(8,128)S(1)} %get-tuple-element.54), channel_id=1, source_target_pairs={{8,0},{16,8},{24,16},{32,24},{40,32},{48,40},{56,48},{9,1},{17,9},... | collective-permute-start | bytes 688136 | tf_op jit(solution)/shard_map/ppermute | solution.py:677
  14.8 7.3 %collective-permute-start.2 = (f32[56,8,128]{2,1,0:T(8,128)S(1)}, f32[56,8,128]{2,1,0:T(8,128)S(1)}, u32[]{:S(2)}, u32[]{:S(2)}) collective-permute-start(f32[56,8,128]{2,1,0:T(8,128)S(1)} %get-tuple-element.55), channel_id=1, source_target_pairs={{0,8},{8,16},{16,24},{24,32},{32,40},{40,48},{48,56},{1,9},{9,17},... | collective-permute-start | bytes 688136 | tf_op jit(solution)/shard_map/ppermute | solution.py:677
  24.1 8.7 %collective-permute-start.4 = (f32[5,80,128]{2,1,0:T(8,128)S(1)}, f32[5,80,128]{2,1,0:T(8,128)S(1)}, u32[]{:S(2)}, u32[]{:S(2)}) collective-permute-start(f32[5,80,128]{2,1,0:T(8,128)S(1)} %get-tuple-element.27), channel_id=1, source_target_pairs={{0,1},{1,2},{2,3},{3,4},{4,5},{5,6},{6,7},{8,9},{9,10},{10,11},{11... | collective-permute-start | bytes 614408 | tf_op jit(solution)/shard_map/ppermute | solution.py:677
  30.1 7.1 %collective-permute-start.5 = (f32[5,80,128]{2,1,0:T(8,128)S(1)}, f32[5,80,128]{2,1,0:T(8,128)S(1)}, u32[]{:S(2)}, u32[]{:S(2)}) collective-permute-start(f32[5,80,128]{2,1,0:T(8,128)S(1)} %get-tuple-element.28), channel_id=1, source_target_pairs={{1,0},{2,1},{3,2},{4,3},{5,4},{6,5},{7,6},{9,8},{10,9},{11,10},{12... | collective-permute-start | bytes 614408 | tf_op jit(solution)/shard_map/ppermute | solution.py:677
  51.9 5.3 %collective-permute-start.6 = (f32[4,32,128]{2,1,0:T(8,128)S(1)}, f32[4,32,128]{2,1,0:T(8,128)S(1)}, u32[]{:S(2)}, u32[]{:S(2)}) collective-permute-start(f32[4,32,128]{2,1,0:T(8,128)S(1)} %get-tuple-element.29.high_quads), channel_id=1, source_target_pairs={{0,64},{64,128},{128,192},{192,256},{256,320},{320,384},{384,448},... | collective-permute-start | bytes 196616 | tf_op jit(solution)/shard_map/ppermute | solution.py:677
  55.9 6.9 %collective-permute-start.7 = (f32[4,32,128]{2,1,0:T(8,128)S(1)}, f32[4,32,128]{2,1,0:T(8,128)S(1)}, u32[]{:S(2)}, u32[]{:S(2)}) collective-permute-start(f32[4,32,128]{2,1,0:T(8,128)S(1)} %get-tuple-element.30.low_quads), channel_id=1, source_target_pairs={{64,0},{128,64},{192,128},{256,192},{320,256},{384,320},{448,384},... | collective-permute-start | bytes 196616 | tf_op jit(solution)/shard_map/ppermute | solution.py:677
  62.8 6.1 %collective-permute-start.8 = (f32[16,16,128]{2,1,0:T(8,128)S(1)}, f32[16,16,128]{2,1,0:T(8,128)S(1)}, u32[]{:S(2)}, u32[]{:S(2)}) collective-permute-start(f32[16,16,128]{2,1,0:T(8,128)S(1)} %pad_maximum_fusion), channel_id=1, source_target_pairs={{0,8},{8,16},{16,24},{24,32},{32,40},{40,48},{48,56},{1,9},{9,17},... | collective-permute-start | bytes 393224 | tf_op jit(solution)/shard_map/ppermute | solution.py:677
  66.9 5.7 %collective-permute-start.9 = (f32[16,16,128]{2,1,0:T(8,128)S(1)}, f32[16,16,128]{2,1,0:T(8,128)S(1)}, u32[]{:S(2)}, u32[]{:S(2)}) collective-permute-start(f32[16,16,128]{2,1,0:T(8,128)S(1)} %pad_maximum_fusion.1), channel_id=1, source_target_pairs={{8,0},{16,8},{24,16},{32,24},{40,32},{48,40},{56,48},{9,1},{17,9},... | collective-permute-start | bytes 393224 | tf_op jit(solution)/shard_map/ppermute | solution.py:677
  72.8 8.4 %collective-permute-start.10 = (f32[8,64,128]{2,1,0:T(8,128)S(1)}, f32[8,64,128]{2,1,0:T(8,128)S(1)}, u32[]{:S(2)}, u32[]{:S(2)}) collective-permute-start(f32[8,64,128]{2,1,0:T(8,128)S(1)} %get-tuple-element.32), channel_id=1, source_target_pairs={{0,1},{1,2},{2,3},{3,4},{4,5},{5,6},{6,7},{8,9},{9,10},{10,11},{11... | collective-permute-start | bytes 786440 | tf_op jit(solution)/shard_map/ppermute | solution.py:677
  78.0 7.7 %collective-permute-start.11 = (f32[8,64,128]{2,1,0:T(8,128)S(1)}, f32[8,64,128]{2,1,0:T(8,128)S(1)}, u32[]{:S(2)}, u32[]{:S(2)}) collective-permute-start(f32[8,64,128]{2,1,0:T(8,128)S(1)} %get-tuple-element.33), channel_id=1, source_target_pairs={{1,0},{2,1},{3,2},{4,3},{5,4},{6,5},{7,6},{9,8},{10,9},{11,10},{12... | collective-permute-start | bytes 786440 | tf_op jit(solution)/shard_map/ppermute | solution.py:677

commit v2 on v1

v2 whole, which is shorter than its diff:
```python
import typing

import jax
import jax.numpy as jnp
from jax import lax
from jax.experimental import pallas as pl
from jax.experimental.pallas import tpu as pltpu
from jax.sharding import PartitionSpec as P


F32 = jnp.float32
BF16 = jnp.bfloat16
COARSE_SWEEPS = 4
COUNT = 8


class Level(typing.NamedTuple):
    level: int
    pairs: int
    rows: int
    first: int
    offset: int
    size: int

    @property
    def scale(self):
        return 4.0**self.level

    @property
    def inverse(self):
        return 0.25**self.level

    @property
    def own(self):
        return self.size // 2

    def shape(self):
        return (self.pairs + 2, self.rows, 128)


L0 = Level(0, 40, 80, 3, 8, 64)
L1 = Level(1, 30, 64, 7, 16, 32)
L2 = Level(2, 14, 32, 3, 8, 16)
L3_OWN = Level(3, 6, 16, 1, 4, 8)
L3 = Level(3, 12, 32, 4, 8, 8)
L4 = Level(4, 16, 32, 0, 0, 32)
L5 = Level(5, 8, 16, 0, 0, 16)
L6 = Level(6, 4, 8, 0, 0, 8)


class Edges(typing.NamedTuple):
    ilo: typing.Any
    ihi: typing.Any
    jlo: typing.Any
    jhi: typing.Any
    klo: typing.Any
    khi: typing.Any


def block_edges():
    ends = []
    for axis in ("gx", "gy", "gz"):
        place = lax.axis_index(axis)
        ends += [place == 0, place == COUNT - 1]
    return Edges(*ends)


def whole_edges():
    yes = lax.axis_index("gx") >= 0
    return Edges(*([yes] * 6))


def lanes_of(shape):
    return lax.broadcasted_iota(jnp.int32, shape, len(shape) - 1)


def rows_of(shape):
    return lax.broadcasted_iota(jnp.int32, shape, len(shape) - 2)


def signed(lane):
    return jnp.where(lane < 96, lane, lane - 128)


def cells_of(shape):
    row = rows_of(shape)
    return (row & 7) * (shape[-2] // 8) + (row >> 3)


def even_mask(rows):
    shape = (rows, 128)
    return ((cells_of(shape) + lanes_of(shape)) & 1) == 0


def even_natural(shape):
    return ((rows_of(shape) + lanes_of(shape)) & 1) == 0


def gather_rows(ref, index, rows, start=0):
    stride = rows // 8
    if stride == 1:
        return ref[index, pl.ds(start, 8), :]
    return jnp.concatenate([ref[index, pl.ds(start + t, 8, stride=stride), :] for t in range(stride)], axis=0)


def scatter_rows(ref, index, value, start=0):
    stride = value.shape[0] // 8
    for t in range(stride):
        ref[index, pl.ds(start + t, 8, stride=stride), :] = value[8 * t : 8 * t + 8]


def row_before(value):
    last = value[value.shape[0] - 8 :]
    first = jnp.where(rows_of((8, 128)) == 0, 0.0, pltpu.roll(last, 1, 0))
    return first if value.shape[0] == 8 else jnp.concatenate([first, value[: value.shape[0] - 8]], axis=0)


def row_after(value):
    last = jnp.where(rows_of((8, 128)) == 7, 0.0, pltpu.roll(value[:8], 7, 0))
    return last if value.shape[0] == 8 else jnp.concatenate([value[8:], last], axis=0)


def fold_rows(value):
    tiles = value.shape[0] // 16
    if tiles == 0:
        raise ValueError("rows")
    return jnp.concatenate([value[16 * t : 16 * t + 8] + value[16 * t + 8 : 16 * t + 16] for t in range(tiles)], axis=0)


def double_rows(even, odd):
    parts = []
    for t in range(even.shape[0] // 8):
        parts += [even[8 * t : 8 * t + 8], odd[8 * t : 8 * t + 8]]
    return jnp.concatenate(parts, axis=0)


def turn(value, shift, axis):
    size = value.shape[axis]
    if isinstance(shift, int):
        shift %= size
        if shift == 0:
            return value
    return pltpu.roll(value, shift, axis)


def bounds(low, high, size):
    return jnp.where(low, 0, -4096), jnp.where(high, size, 4096)


def set_coefficients(lv, edges, c_ref, d_ref):
    shape = (lv.rows, 128)
    row = cells_of(shape) - lv.offset
    lane = signed(lanes_of(shape))
    row_low, row_high = bounds(edges.jlo, edges.jhi, lv.size)
    lane_low, lane_high = bounds(edges.klo, edges.khi, lv.size)
    inside = (row >= row_low) & (row < row_high) & (lane >= lane_low) & (lane < lane_high)
    diagonal = 6.0 + jnp.where(row == row_low, 1.0, 0.0) + jnp.where(row == row_high - 1, 1.0, 0.0)
    diagonal = diagonal + jnp.where(lane == lane_low, 1.0, 0.0) + jnp.where(lane == lane_high - 1, 1.0, 0.0)
    even = jnp.where(even_mask(lv.rows), 1.0, 0.0)
    for index, extra in enumerate((0.0, even, 1.0 - even)):
        d_ref[index] = diagonal + extra
        c_ref[index] = jnp.where(inside, 1.0 / (diagonal + extra), 0.0)
    c_ref[3] = jnp.zeros(shape, F32)


def kind(lv, edges, p, red):
    last = lv.first + lv.own - 1
    low, high = (1, 2) if red else (2, 1)
    if isinstance(p, int):
        if p in (lv.first, last):
            return jnp.where(edges.ilo, low, 0) if p == lv.first else jnp.where(edges.ihi, high, 0)
        return 0 if lv.first < p < last else jnp.where(edges.ilo if p < lv.first else edges.ihi, 3, 0)
    inner = jnp.where((p == lv.first) & edges.ilo, low, jnp.where((p == last) & edges.ihi, high, 0))
    return jnp.where(((p < lv.first) & edges.ilo) | ((p > last) & edges.ihi), 3, inner)


def loop(low, high, body, width=0):
    count = high - low
    width = count if width == 0 else min(width, count)

    def step(n, carry):
        for k in range(width):
            body(low + n * width + k)
        return carry

    if count // width > 1:
        lax.fori_loop(0, count // width, step, 0)
        done = count // width * width
    else:
        done = 0
    for p in range(low + done, high):
        body(p)


def group(rows):
    return max(1, 180 // (rows // 8))


def around(ref, p, even, red):
    value = ref[p + 1]
    before, after = ref[p], ref[p + 2]
    total = value + (jnp.where(even, before, after) if red else jnp.where(even, after, before))
    total = total + (row_before(value) + row_after(value))
    return total + (turn(value, 1, 1) + turn(value, 127, 1))


def relax_at(lv, edges, c_ref, other, source, dest, p, red, even):
    total = around(other, p, even, red) + (source[p + 1] if lv.level == 0 else lv.scale * source[p + 1])
    dest[p + 1] = total * c_ref[kind(lv, edges, p, red)]


def relax(lv, edges, c_ref, other, source, dest, low, high, red):
    even = even_mask(lv.rows)
    loop(low, high, lambda p: relax_at(lv, edges, c_ref, other, source, dest, p, red, even), group(lv.rows))


def relax_zero(lv, edges, c_ref, source, dest, low, high):
    def body(p):
        dest[p + 1] = lv.scale * source[p + 1] * c_ref[kind(lv, edges, p, True)]

    loop(low, high, body, group(lv.rows))


def gap(lv, d, value, total):
    return d * value - total if lv.level == 0 else lv.inverse * (d * value - total)


def black_rest_at(lv, edges, c_ref, d_ref, red, source, dest, rest, p, even):
    total = around(red, p, even, False)
    g = source[p + 1]
    at = kind(lv, edges, p, False)
    value = (total + (g if lv.level == 0 else lv.scale * g)) * c_ref[at]
    dest[p + 1] = value
    rest[p + 1] = g - gap(lv, d_ref[jnp.minimum(at, 2)], value, total)


def relax_black_rest(lv, edges, c_ref, d_ref, red, source, dest, rest, low, high):
    even = even_mask(lv.rows)
    loop(low, high, lambda p: black_rest_at(lv, edges, c_ref, d_ref, red, source, dest, rest, p, even), group(lv.rows))


def red_rest(lv, edges, d_ref, source, red, black, p, even):
    d = d_ref[jnp.minimum(kind(lv, edges, p, True), 2)]
    return source[p + 1] - gap(lv, d, red[p + 1], around(black, p, even, True))


def clear_guards(*refs):
    for ref in refs:
        ref[0] = jnp.zeros(ref.shape[1:], F32)
        ref[ref.shape[0] - 1] = jnp.zeros(ref.shape[1:], F32)


def split_dot(value, weights):
    high = value.astype(BF16)
    low = (value - high.astype(F32)).astype(BF16)
    return jnp.dot(jnp.concatenate([high, low], axis=1), weights, preferred_element_type=F32)


def halving_weights(own_lanes):
    shape = (256, 128)
    fine = signed(rows_of(shape) & 127)
    coarse = signed(lanes_of(shape))
    hit = (fine >> 1) == coarse
    if own_lanes:
        hit = hit & (fine >= 0) & (fine < own_lanes)
    return jnp.where(hit, 0.125, 0.0).astype(BF16)


def doubling_weights(size, low, high):
    shape = (256, 256)
    coarse = signed(rows_of(shape) & 127)
    lane = lanes_of(shape)
    fine = signed(lane & 127)
    parent = fine >> 1
    beside = parent + jnp.where((fine & 1) == 1, 1, -1)
    beyond = ((beside == -1) & low) | ((beside == size) & high)
    centre = jnp.where(coarse == parent, 0.25, 0.0)
    neighbour = jnp.where(coarse == beside, 0.25, 0.0)
    mixed = jnp.where(beyond, 0.0, centre + neighbour)
    return jnp.where(lane < 128, mixed, centre).astype(BF16)


def rest_fold_at(lv, edges, d_ref, g_red, red, black, rest, low, z_ref, p, even):
    z_ref[p - low] = fold_rows(rest[p + 1] + red_rest(lv, edges, d_ref, g_red, red, black, p, even))


def restrict(lv, edges, d_ref, g_red, red, black, rest, low, count, z_ref, out_ref, weights):
    even = even_mask(lv.rows)
    loop(
        low, low + count,
        lambda p: rest_fold_at(lv, edges, d_ref, g_red, red, black, rest, low, z_ref, p, even), group(lv.rows),
    )
    halve(lv, count, z_ref, out_ref, weights)


def halve(lv, count, z_ref, out_ref, weights):
    half = lv.rows // 2
    chunk = max(c for c in range(1, count + 1) if count % c == 0 and (c * half <= 320 or c == 1))

    def product(n):
        value = z_ref[pl.ds(n * chunk, chunk)].reshape(chunk * half, 128)
        out_ref[pl.ds(n * chunk, chunk)] = split_dot(value, weights[...]).reshape(chunk, half, 128)

    loop(0, count // chunk, product)


def colour_planes(planes, pairs, red, black):
    even = even_mask(planes.shape[1])

    def body(p):
        low, high = planes[2 * p], planes[2 * p + 1]
        red[p + 1] = jnp.where(even, low, high)
        black[p + 1] = jnp.where(even, high, low)

    loop(0, pairs, body, 8)


def whole_planes(lv, red, black, pair_low, pairs, e_ref):
    even = even_mask(lv.rows)

    def body(t):
        r, b = red[pair_low + t + 1], black[pair_low + t + 1]
        e_ref[2 * t] = jnp.where(even, r, b)
        e_ref[2 * t + 1] = jnp.where(even, b, r)

    loop(0, pairs, body, 8)


def window_planes(lv, red, black, pair_low, pairs, row_low, natural, e_ref):
    even = even_mask(lv.rows)
    rows = e_ref.shape[1]

    def body(t):
        r, b = red[pair_low + t + 1], black[pair_low + t + 1]
        scatter_rows(natural, 2 * t, jnp.where(even, r, b))
        scatter_rows(natural, 2 * t + 1, jnp.where(even, b, r))

    def again(t):
        e_ref[t] = gather_rows(natural, t, rows, row_low)

    loop(0, pairs, body, 4)
    loop(0, 2 * pairs, again, 8)


def prolong(e_ref, count, plane_zero, size, edges, weights, mixed, plain):
    rows = e_ref.shape[1]
    chunk = max(c for c in range(1, count + 1) if count % c == 0 and (c * rows <= 320 or c == 1))

    def body(n):
        at = pl.ds(n * chunk, chunk)
        both = split_dot(e_ref[at].reshape(chunk * rows, 128), weights[...])
        mixed[at] = both[:, :128].reshape(chunk, rows, 128)
        plain[at] = both[:, 128:].reshape(chunk, rows, 128)

    loop(0, count // chunk, body)
    if plane_zero > 0:
        pl.when(edges.ilo)(lambda: plain.__setitem__(plane_zero - 1, -plain[plane_zero]))
    last = plane_zero + size - 1
    if last + 1 < count:
        pl.when(edges.ihi)(lambda: plain.__setitem__(last + 1, -plain[last]))


def correct(lv, edges, c_ref, kept, mixed, plain, row_zero, plane_zero, dest, low, high):
    body = correct_at(lv, edges, c_ref, kept, mixed, plain, row_zero, plane_zero, dest)
    loop(low, high, body, group(lv.rows))


def correct_at(lv, edges, c_ref, kept, mixed, plain, row_zero, plane_zero, dest):
    even = even_mask(lv.rows)
    half = lv.rows // 2
    row = cells_of((half, 128)) - row_zero
    at_low = (row == 0) & edges.jlo
    at_high = (row == lv.size // 2 - 1) & edges.jhi

    def body(p):
        t = p - lv.first + plane_zero
        value, near = plain[t], mixed[t]
        before = near + jnp.where(at_low, -value, row_before(value))
        after = near + jnp.where(at_high, -value, row_after(value))
        up, down = plain[t + 1], plain[t - 1]
        step = double_rows(before, after) + jnp.where(even, double_rows(up, up), double_rows(down, down))
        c = c_ref[kind(lv, edges, p, False)]
        dest[p + 1] = jnp.where(c > 0.0, kept[p + 1] + step, 0.0)

    return body


def compact_kernel(guess, source, x_ref, y_ref):
    even = ((rows_of((64, 64)) + lanes_of((64, 64))) & 1) == 0

    def body(u):
        blacks = []
        for s in range(2):
            p = 2 * u + s
            low, high = guess[2 * p], guess[2 * p + 1]
            f_low, f_high = source[2 * p], source[2 * p + 1]
            x_ref[p] = jnp.concatenate([jnp.where(even, high, low), jnp.where(even, f_low, f_high)], axis=1)
            blacks.append(jnp.where(even, f_high, f_low))
        y_ref[u] = jnp.concatenate(blacks, axis=1)

    loop(0, 16, body, 2)


def pack_kernel(ib, ia, x, y, jb, ja, xf, yf, ku, kd):
    zero = jnp.zeros((80, 128), F32)
    for p in range(3):
        xf[p, 8:72] = ib[p]
        xf[35 + p, 8:72] = ia[p]
    loop(0, 32, lambda p: xf.__setitem__((p + 3, slice(8, 72)), x[p]), 4)
    yf[0, 8:72] = ib[3]
    yf[17, 8:72] = ia[3]
    loop(0, 16, lambda p: yf.__setitem__((p + 1, slice(8, 72)), y[p]), 4)

    tile = jnp.zeros((8, 128), F32)
    for p in range(38):
        xf[p, 0:8] = tile
        xf[p, 3:8] = jb[5 * p : 5 * p + 5]
        xf[p, 72:80] = tile
        xf[p, 72:77] = ja[5 * p : 5 * p + 5]
    for p in range(18):
        yf[p, 0:8] = tile
        yf[p, 5:8] = jb[190 + 3 * p : 193 + 3 * p]
        yf[p, 72:80] = tile
        yf[p, 72:75] = ja[190 + 3 * p : 193 + 3 * p]
    for p in (38, 39):
        xf[p] = zero
    for p in range(18, 24):
        yf[p] = zero
    lane = lanes_of((80, 128))
    for u in range(5):
        down, up, up_y = zero, zero, zero
        for s in range(8):
            value = turn(xf[8 * u + s], 8 * s, 1)
            place = (lane - 8 * s) & 127
            down = jnp.where((place < 5) | ((place >= 64) & (place < 68)), value, down)
            up = jnp.where(((place >= 59) & (place < 64)) | (place >= 124), value, up)
            if 8 * u + s < 18:
                value = turn(yf[8 * u + s], 8 * s + 5, 1)
                down = jnp.where(place_y(lane, s, 0), value, down)
                up_y = jnp.where(place_y(lane, s, 61), value, up_y)
        kd[u] = down
        ku[u] = up + turn(up_y, -2, 1) if u < 3 else up


def place_y(lane, s, start):
    place = (lane - 8 * s - 5) & 63
    return (place >= start) & (place < start + 3)


def rows_kernel(ib, ia, guess_low, guess_high, source_low, source_high, up, down):
    even = even_natural((8, 64))
    for out, guess, source, low, x_at, y_at in (
        (down, guess_low, source_low, 0, 0, 0),
        (up, guess_high, source_high, 56, 3, 5),
    ):
        blacks = []
        for p in range(38):
            if 3 <= p < 35:
                n = 2 * p - 6
                first, second, f_first, f_second = guess[n], guess[n + 1], source[n], source[n + 1]
                value = jnp.concatenate(
                    [jnp.where(even, second, first), jnp.where(even, f_first, f_second)], axis=1
                )
                blacks.append(jnp.where(even, f_second, f_first))
            else:
                value = ib[p, low : low + 8] if p < 3 else ia[p - 35, low : low + 8]
            out[5 * p : 5 * p + 5] = value[x_at : x_at + 5]
        for p in range(18):
            if p == 0 or p == 17:
                value = (ib if p == 0 else ia)[3, low : low + 8]
            else:
                value = jnp.concatenate(blacks[2 * p - 2 : 2 * p], axis=1)
            out[190 + 3 * p : 193 + 3 * p] = value[y_at : y_at + 3]
        out[244:248] = jnp.zeros((4, 128), F32)


def spread_kernel(xf, yf, black, g_red, g_black, c_ref, d_ref, weights):
    set_coefficients(L0, block_edges(), c_ref, d_ref)
    weights[...] = halving_weights(64)
    zero = jnp.zeros((80, 128), F32)
    own = lanes_of((80, 128)) < 64

    def first(p):
        value = gather_rows(xf, p, 80)
        black[p + 1] = jnp.where(own, value, 0.0)
        g_red[p + 1] = jnp.where(own, turn(value, 64, 1), 0.0)

    loop(0, 40, first, 4)

    def second(p):
        value = gather_rows(yf, p, 80)
        g_black[2 * p + 2] = jnp.where(own, value, 0.0)
        g_black[2 * p + 3] = jnp.where(own, turn(value, 64, 1), 0.0)

    loop(0, 18, second, 4)
    for q in (0, 1, 38, 39, 40, 41):
        g_black[q] = zero
    clear_guards(black, g_red)


def fine_kernel(
    black0, g_red0, g_black0, kb, ka, c_ref, d_ref, weights, v_black, g_red, g_black, low_quads, high_quads,
    black, red, rest, z_ref, planes, natural,
):
    edges = block_edges()
    zero = jnp.zeros((80, 128), F32)
    lane = lanes_of((80, 128))

    even = even_mask(80)

    def sides(u):
        below = jnp.where(edges.klo, 0.0, gather_rows(kb, u, 80))
        return below, jnp.where(edges.khi, 0.0, gather_rows(ka, u, 80))

    def merge(p):
        below, above = sides(p // 8)
        turned = 8 * (p % 8)
        place = (lane - turned) & 127
        edge = jnp.where(place < 5, above, jnp.where((place >= 59) & (place < 64), below, 0.0))
        black[p + 1] = black0[p + 1] + turn(edge, 64 - turned, 1)
        edge = jnp.where((place >= 64) & (place < 68), above, jnp.where(place >= 124, below, 0.0))
        g_red[p + 1] = g_red0[p + 1] + turn(edge, -turned, 1)

    def merge_black(n):
        below, above = sides(n // 8)
        below = turn(below, 2, 1)
        turned = 8 * (n % 8)
        place = (lane - turned) & 127
        edge = jnp.where((place >= 5) & (place < 8), above, jnp.where((place >= 66) & (place < 69), below, 0.0))
        g_black[2 * n + 2] = g_black0[2 * n + 2] + turn(edge, 59 - turned, 1)
        edge = jnp.where((place >= 69) & (place < 72), above, jnp.where((place >= 2) & (place < 5), below, 0.0))
        g_black[2 * n + 3] = g_black0[2 * n + 3] + turn(edge, -5 - turned, 1)

    for q in (0, 1, 38, 39, 40, 41):
        g_black[q] = zero
    for ref in (black, g_red):
        for q in (0, 39, 40, 41):
            ref[q] = zero
    for ref in (red, v_black):
        for q in (0, 1, 38, 39, 40, 41):
            ref[q] = zero
    for n in range(44):
        if n < 38:
            merge(n)
        if n % 2 == 0 and n < 36:
            merge_black(n // 2)
        if 1 <= n - 2 < 37:
            relax_at(L0, edges, c_ref, black, g_red, red, n - 2, True, even)
        if 1 <= n - 4 < 37:
            black_rest_at(L0, edges, c_ref, d_ref, red, g_black, v_black, rest, n - 4, even)
        if 3 <= n - 6 < 35:
            rest_fold_at(L0, edges, d_ref, g_red, red, v_black, rest, 3, z_ref, n - 6, even)
    halve(L0, 32, z_ref, planes, weights)

    def quad(q):
        total = planes[4 * q]
        for m in range(1, 4):
            total = total + turn(planes[4 * q + m], 32 * m, 1)
        scatter_rows(natural, q, total)
        return natural[q, 4:36]

    for q in range(4):
        low_quads[q] = quad(q)
        high_quads[q] = quad(q + 4)


def pack_quads_kernel(ib, ia, low_quads, high_quads, jb, ja, qf, ku, kd):
    for index, part in enumerate((ib, low_quads, high_quads, ia)):
        for q in range(4):
            qf[4 * index + q, 16:48] = part[q]
    for q in range(16):
        qf[q, 0:16] = jb[q]
        qf[q, 48:64] = ja[q]
    low_half = (lanes_of((64, 128)) & 31) < 16
    for u in range(8):
        first, second = qf[2 * u], qf[2 * u + 1]
        kd[u] = turn(jnp.where(low_half, first, turn(second, 16, 1)), 32, 1)
        ku[u] = turn(jnp.where(low_half, turn(first, -16, 1), second), -32, 1)


WINDOWS = (L1, L2, L3_OWN, L3)
WHOLES = (L4, L5, L6)
DOUBLINGS = ((32, False), (16, False), (8, False), (4, False), (16, True), (8, True))


def geometry_kernel(after, *refs):
    edges, whole = block_edges(), whole_edges()
    for index, lv in enumerate(WINDOWS + WHOLES):
        set_coefficients(lv, edges if lv in WINDOWS else whole, refs[2 * index], refs[2 * index + 1])
    refs = refs[2 * len(WINDOWS + WHOLES) :]
    refs[0][...] = halving_weights(0)
    for n, (size, is_whole) in enumerate(DOUBLINGS):
        at = whole if is_whole else edges
        refs[1][n] = doubling_weights(size, at.klo, at.khi)


def middle_kernel(
    qf, kb, ka, c1, d1, c2, d2, c3, d3, weights, v1, gr1, gb1, v2, gr2, gb2, message,
    red1, y1, z1, p1, red2, y2, z2, p2, gr3, gb3, red3, black3, y3, z3, p3, natural,
):
    edges = block_edges()
    lane = lanes_of((64, 128))
    even = even_mask(64)

    def unpack(u):
        below = jnp.where(edges.klo, 0.0, gather_rows(kb, u, 64))
        above = jnp.where(edges.khi, 0.0, gather_rows(ka, u, 64))
        sides = ((turn(below, 16, 1), above), (below, turn(above, -16, 1)))
        for h in range(2):
            value = gather_rows(qf, 2 * u + h, 64)
            left, right = sides[h]
            for t in range(2):
                both = []
                for m in (2 * t, 2 * t + 1):
                    place = (lane - 32 * m) & 127
                    edge = jnp.where(place < 48, right, jnp.where(place >= 112, left, 0.0))
                    both.append(turn(jnp.where(place < 32, value, edge), -32 * m, 1))
                index = 4 * u + 2 * h + t
                gr1[index] = jnp.where(even, both[0], both[1])
                gb1[index] = jnp.where(even, both[1], both[0])

    clear_guards(red1, v1)
    for n in range(36):
        if n % 4 == 0 and n < 32:
            unpack(n // 4)
        p = n - 1
        if 0 <= p < 30:
            red1[p + 1] = L1.scale * gr1[p + 1] * c1[kind(L1, edges, p, True)]
        if 0 <= n - 3 < 30:
            black_rest_at(L1, edges, c1, d1, red1, gb1, v1, y1, n - 3, even)
        if 1 <= n - 5 < 29:
            rest_fold_at(L1, edges, d1, gr1, red1, v1, y1, 1, z1, n - 5, even)
    halve(L1, 28, z1, p1, weights)
    colour_planes(p1, 14, gr2, gb2)
    clear_guards(red2, v2, gr2, gb2)
    relax_zero(L2, edges, c2, gr2, red2, 0, 14)
    relax_black_rest(L2, edges, c2, d2, red2, gb2, v2, y2, 0, 14)
    restrict(L2, edges, d2, gr2, red2, v2, y2, 1, 12, z2, p2, weights)
    colour_planes(p2, 6, gr3, gb3)
    clear_guards(red3, black3)
    relax_zero(L3_OWN, edges, c3, gr3, red3, 0, 6)
    relax_black_rest(L3_OWN, edges, c3, d3, red3, gb3, black3, y3, 0, 6)
    restrict(L3_OWN, edges, d3, gr3, red3, black3, y3, 1, 4, z3, p3, weights)
    lane = lanes_of((8, 128))
    row = rows_of((8, 128))
    third = jnp.zeros((8, 128), F32)
    for i in range(8):
        scatter_rows(natural, i, p2[i + 2])
        third = third + turn(jnp.where(lane < 8, natural[i, 4:12], 0.0), 8 * i, 1)
    folded = third + turn(turn(third, 4, 0), 64, 1)
    blocks = jnp.zeros((8, 128), F32)
    for i in range(4):
        blocks = blocks + turn(jnp.where(lane < 4, p3[i], 0.0), 16 * i, 1)
    fourth = jnp.zeros((8, 128), F32)
    for r in range(4):
        fourth = jnp.where((lane & 15) >> 2 == r, turn(turn(blocks, 4 * r, 1), -2 - r, 0), fourth)

    def store(n):
        for r in range(4):
            message[n, r] = folded[r : r + 1]
        message[n, 4] = fourth[0:1]

    loop(0, 64, store, 8)


def plane_kernel(tiles, message, near, rows, grid, blocks):
    x, y, z = (lax.axis_index(axis) for axis in ("gx", "gy", "gz"))
    shape = (8, 128)
    lane, row = lanes_of(shape), rows_of(shape)

    for n in range(64):
        rows[n : n + 1] = tiles[n, 4]
    parts = [jnp.zeros(shape, F32)] * 4
    for n in range(8):
        value = rows[pl.ds(n, 8, stride=8), :]
        here = (lane & 31) >> 2 == n
        for r in range(4):
            index = (lane >> 5) * 16 + 4 * r + (lane & 3)
            parts[r] = jnp.where(here, jnp.take_along_axis(value, index, axis=1), parts[r])
    for r in range(4):
        grid[pl.ds(r, 8, stride=4), :] = parts[r]

    lane = signed(lane)
    for dy in range(3):
        sides = []
        for dz in range(3):
            yy, zz = y + (dy - 1), z + (dz - 1)
            inside = (yy >= 0) & (yy < COUNT) & (zz >= 0) & (zz < COUNT)
            index = jnp.clip(yy, 0, COUNT - 1) * COUNT + jnp.clip(zz, 0, COUNT - 1)
            for r in range(4):
                blocks[3 * dy + dz, r : r + 1] = tiles[index, r]
            value = blocks[3 * dy + dz]
            value = jnp.where(row < 4, value, turn(turn(value, 4, 0), 64, 1))
            sides.append(jnp.where(inside, value, 0.0))
        for i in range(8):
            total = jnp.zeros(shape, F32)
            for dz in range(3):
                hit = (lane >= 8 * (dz - 1)) & (lane < 8 * dz)
                total = jnp.where(hit, turn(sides[dz], 8 * (dz - 1) - 8 * i, 1), total)
            near[i, 8 * dy : 8 * dy + 8] = total

    wide = lanes_of((24, 128))
    ends = []
    for first in (2, 0):
        total = jnp.zeros((24, 128), F32)
        for n in range(6):
            hit = (wide >= 20 * n) & (wide < 20 * n + 20)
            total = jnp.where(hit, turn(near[first + n], 20 * n + 6, 1), total)
        ends.append(total)
    for n in range(COUNT):
        message[n, 0:32] = grid[...]
        message[n, 32:56] = jnp.where(x < n, ends[0], ends[1])


def coarse_kernel(
    tiles, near, v2, gr2, gb2, v1, gr1, gb1, v0, gr0, gb0, c0, d0, c1, c2, c3, c4, d4, c5, d5, c6, halving, doubling, out, rest,
    gr4, gb4, red4, v4, y4, z4, p4, gr5, gb5, red5, v5, y5, z5, p5, gr6, gb6, red6, v6, full,
    gr3, gb3, red3, v3, b3, b2, red2, b1, red1, b0, red0, y0, e_ref, mixed, plain, natural, last, out_held, rest_held, sems,
):
    edges = block_edges()
    whole = whole_edges()
    x, y, z = (lax.axis_index(axis) for axis in ("gx", "gy", "gz"))

    lane = signed(lanes_of((24, 128)))
    even = even_natural((24, 128))
    empty = jnp.zeros((24, 128), F32)

    def put(index, low, high):
        natural[index, 0:24] = jnp.where(even, low, high)
        natural[index + 12, 0:24] = jnp.where(even, high, low)

    for n in range(4):
        put(4 + n, near[2 * n], near[2 * n + 1])
    put(0, empty, empty)
    put(11, empty, empty)
    for at, first in ((x - 1, 1), (x + 1, 8)):
        inside = (at >= 0) & (at < COUNT)
        value = jnp.where(inside, tiles[jnp.clip(at, 0, COUNT - 1), 32:56], 0.0)
        planes = [jnp.where((lane >= -6) & (lane < 14), turn(value, -20 * n - 6, 1), 0.0) for n in range(6)]
        for n in range(3):
            put(first + n, planes[2 * n], planes[2 * n + 1])
    for n in range(24):
        natural[n, 24:32] = jnp.zeros((8, 128), F32)
    for n in range(12):
        gr3[n + 1] = gather_rows(natural, n, 32)
        gb3[n + 1] = gather_rows(natural, n + 12, 32)
    clear_guards(red3, v3)
    relax_zero(L3, edges, c3, gr3, red3, 0, 12)
    relax(L3, edges, c3, red3, gb3, v3, 0, 12, False)

    lane = lanes_of((32, 128))
    even32 = even_mask(32)
    zero = jnp.zeros((8, 128), F32)

    def place(n):
        value = gather_rows(tiles, n, 32)
        for t in range(2):
            low = jnp.where(lane < 32, turn(value, -64 * t, 1), 0.0)
            high = jnp.where(lane < 32, turn(value, -64 * t - 32, 1), 0.0)
            index = 2 * n + t + 1
            gr4[index] = jnp.where(even32, low, high)
            gb4[index] = jnp.where(even32, high, low)

    loop(0, 8, place, 4)
    clear_guards(red4, v4, gr4, gb4)
    relax_zero(L4, whole, c4, gr4, red4, 0, 16)
    relax_black_rest(L4, whole, c4, d4, red4, gb4, v4, y4, 0, 16)
    restrict(L4, whole, d4, gr4, red4, v4, y4, 0, 16, z4, p4, halving)
    colour_planes(p4, 8, gr5, gb5)
    clear_guards(red5, v5, gr5, gb5)
    relax_zero(L5, whole, c5, gr5, red5, 0, 8)
    relax_black_rest(L5, whole, c5, d5, red5, gb5, v5, y5, 0, 8)
    restrict(L5, whole, d5, gr5, red5, v5, y5, 0, 8, z5, p5, halving)
    colour_planes(p5, 4, gr6, gb6)
    clear_guards(red6, v6)
    relax_zero(L6, whole, c6, gr6, red6, 0, 4)
    relax(L6, whole, c6, red6, gb6, v6, 0, 4, False)
    for _ in range(COARSE_SWEEPS - 1):
        relax(L6, whole, c6, v6, gr6, red6, 0, 4, True)
        relax(L6, whole, c6, red6, gb6, v6, 0, 4, False)

    def ascend(coarse, fine, c, w, coarse_red, coarse_black, kept, g_red, g_black, red):
        count = coarse.size
        e, rows = e_ref.at[0:count, 0:count], slice(0, count)
        n, p = mixed.at[0 : count + 2, rows], plain.at[0 : count + 2, rows]
        whole_planes(coarse, coarse_red, coarse_black, 0, coarse.pairs, e)
        prolong(e, count, 0, count, whole, w, mixed.at[1 : count + 1, rows], plain.at[1 : count + 1, rows])
        p[0] = -p[1]
        p[count + 1] = -p[count]
        correct(fine, whole, c, kept, n, p, 0, 1, kept, 0, fine.pairs)
        relax(fine, whole, c, kept, g_red, red, 0, fine.pairs, True)
        relax(fine, whole, c, red, g_black, kept, 0, fine.pairs, False)

    ascend(L6, L5, c5, doubling.at[5], red6, v6, v5, gr5, gb5, red5)
    ascend(L5, L4, c4, doubling.at[4], red5, v5, v4, gr4, gb4, red4)

    even = even_mask(32)
    for t in (0, 1, 2, 3, 36, 37, 38, 39):
        full[t] = jnp.zeros((48, 128), F32)

    def expand(t):
        r, b = red4[t + 1], v4[t + 1]
        for n, value in ((2 * t + 4, jnp.where(even, r, b)), (2 * t + 5, jnp.where(even, b, r))):
            full[n, 0:8] = zero
            scatter_rows(full, n, value, 8)
            full[n, 40:48] = zero

    loop(0, 16, expand, 4)

    def cut(t):
        rows = gather_rows(full, 4 * x + t, 16, 4 * y + 4)
        e_ref[t, 0:16] = pltpu.roll(rows, (128 - 4 * z) & 127, 1)

    loop(0, 12, cut)

    def lift(index, fine, c, count, rows, plane_zero, row_zero, size, kept, dest, low, high):
        e = e_ref.at[0:count, 0:rows]
        n, p = mixed.at[0:count, 0:rows], plain.at[0:count, 0:rows]
        prolong(e, count, plane_zero, size, edges, doubling.at[index], n, p)
        correct(fine, edges, c, kept, n, p, row_zero, plane_zero, dest, low, high)

    def smooth(lv, c, black, g_red, g_black, red, low, high, low2, high2):
        relax(lv, edges, c, black, g_red, red, low, high, True)
        relax(lv, edges, c, red, g_black, black, low2, high2, False)

    lift(3, L3, c3, 12, 16, 4, 4, 4, v3, b3, 1, 11)
    clear_guards(b3, red3)
    smooth(L3, c3, b3, gr3, gb3, red3, 2, 10, 2, 10)

    window_planes(L3, red3, b3, 2, 8, 4, natural.at[0:16, 0:32], e_ref.at[0:16, 0:16])
    lift(2, L2, c2, 16, 16, 4, 4, 8, v2, b2, 0, 14)
    clear_guards(b2, red2)
    smooth(L2, c2, b2, gr2, gb2, red2, 1, 13, 1, 13)

    whole_planes(L2, red2, b2, 1, 12, e_ref.at[0:24, 0:32])
    e = e_ref.at[0:24, 0:32]
    n, p = mixed.at[0:24, 0:32], plain.at[0:24, 0:32]
    prolong(e, 24, 4, 16, edges, doubling.at[1], n, p)
    correct1 = correct_at(L1, edges, c1, v1, n, p, 8, 4, b1)
    for index in (5, 26):
        b1[index] = jnp.zeros(b1.shape[1:], F32)
    even1 = even_mask(64)
    for n in range(5, 29):
        if n < 25:
            correct1(n)
        if 5 <= n - 2 < 25:
            relax_at(L1, edges, c1, b1, gr1, red1, n - 2, True, even1)
        if 6 <= n - 4 < 24:
            relax_at(L1, edges, c1, red1, gb1, b1, n - 4, False, even1)

    window_planes(L1, red1, b1, 5, 20, 12, natural, e_ref.at[0:40, 0:40])
    e = e_ref.at[0:40, 0:40]
    n, p = mixed.at[0:40, 0:40], plain.at[0:40, 0:40]
    prolong(e, 40, 4, 32, edges, doubling.at[0], n, p)
    correct0 = correct_at(L0, edges, c0, v0, n, p, 4, 4, b0)
    b0[1] = jnp.zeros(b0.shape[1:], F32)
    b0[38] = jnp.zeros(b0.shape[1:], F32)
    even0 = even_mask(80)
    copies = []

    def send(held, target, n):
        copy = pltpu.make_async_copy(held.at[pl.ds(8 * n, 8)], target.at[pl.ds(8 * n, 8)], sems.at[len(copies)])
        copy.start()
        copies.append(copy)

    def store(held, p, r, b):
        for n, value in ((0, jnp.where(even0, r, b)), (1, jnp.where(even0, b, r))):
            scatter_rows(last, 2 * (p & 7) + n, value)
            held[2 * p - 6 + n] = last[2 * (p & 7) + n, 8:72, 0:64]

    for n in range(1, 43):
        if n < 37:
            correct0(n)
        if 1 <= n - 2 < 37:
            relax_at(L0, edges, c0, b0, gr0, red0, n - 2, True, even0)
        p = n - 4
        if 2 <= p < 36:
            black_rest_at(L0, edges, c0, d0, red0, gb0, b0, y0, p, even0)
        if 3 <= p < 35:
            store(out_held, p, red0[p + 1], b0[p + 1])
            if p % 4 == 2:
                send(out_held, out, p // 4 - 1)
        p = n - 6
        if 3 <= p < 35:
            store(rest_held, p, red_rest(L0, edges, d0, gr0, red0, b0, p, even0), y0[p + 1])
            if p % 4 == 2:
                send(rest_held, rest, p // 4 - 1)
    for copy in copies:
        copy.wait()


def struct(*shape):
    return jax.ShapeDtypeStruct(shape, F32)


def call(kernel, outs, scratch, flops=2_000_000, out_space=pltpu.VMEM, semaphores=0):
    space = pl.BlockSpec(memory_space=pltpu.VMEM)
    extra = [pltpu.SemaphoreType.DMA((semaphores,))] if semaphores else []

    def run(*args):
        return pl.pallas_call(
            kernel,
            out_shape=outs,
            in_specs=[space] * len(args),
            out_specs=[pl.BlockSpec(memory_space=out_space)] * len(outs),
            scratch_shapes=[pltpu.VMEM(shape, F32) for shape in scratch] + extra,
            compiler_params=pltpu.CompilerParams(vmem_limit_bytes=40 * 2**20),
            cost_estimate=pl.CostEstimate(flops=flops, bytes_accessed=1_000_000, transcendentals=0),
        )(*args)

    return run


def pair(to_next, to_before, axis, ring=False):
    up = [(i, (i + 1) % COUNT) for i in range(COUNT if ring else COUNT - 1)]
    down = [(j, i) for i, j in up]
    after = lax.ppermute(to_before, axis, down)
    before = lax.ppermute(to_next, axis, up)
    return before, after


def face(guess, source, start, first):
    even = ((lax.broadcasted_iota(jnp.int32, (64, 64), 0) + lax.broadcasted_iota(jnp.int32, (64, 64), 1)) & 1) == 0
    low, high = guess[start : start + 6 : 2], guess[start + 1 : start + 6 : 2]
    f_low, f_high = source[start : start + 6 : 2], source[start + 1 : start + 6 : 2]
    red = jnp.where(even, f_low, f_high)
    black = jnp.where(even, f_high, f_low)
    mixed = jnp.concatenate([jnp.where(even, high, low), red], axis=2)
    return jnp.concatenate([mixed, jnp.concatenate([black[first : first + 1], black[first + 1 : first + 2]], axis=2)], axis=0)


def coefficient_shapes(*levels):
    shapes = []
    for lv in levels:
        shapes += [struct(4, lv.rows, 128), struct(3, lv.rows, 128)]
    return shapes


def per_device(right_side, guess):
    ib, ia = pair(face(guess, right_side, 58, 1), face(guess, right_side, 0, 0), "gx")
    x, y = call(compact_kernel, (struct(32, 64, 128), struct(16, 64, 128)), [])(guess, right_side)

    up, down = call(rows_kernel, (struct(248, 128), struct(248, 128)), [])(
        ib, ia, guess[:, 0:8], guess[:, 56:64], right_side[:, 0:8], right_side[:, 56:64]
    )
    jb, ja = pair(up, down, "gy")
    xf, yf, ku, kd = call(
        pack_kernel, (struct(40, 80, 128), struct(24, 80, 128), struct(5, 80, 128), struct(5, 80, 128)), []
    )(ib, ia, x, y, jb, ja)
    kb, ka = pair(ku, kd, "gz", True)
    fine = L0.shape()
    field = struct(*fine)
    weights = jax.ShapeDtypeStruct((256, 128), BF16)
    black, g_red, g_black, c0, d0, w0 = call(
        spread_kernel, (field, field, field, *coefficient_shapes(L0), weights), []
    )(xf, yf)
    v0, gr0, gb0, low_quads, high_quads = call(
        fine_kernel,
        (field, field, field, struct(4, 32, 128), struct(4, 32, 128)),
        [fine, fine, fine, (32, 40, 128), (32, 40, 128), (8, 40, 128)],
    )(black, g_red, g_black, kb, ka, c0, d0, w0)

    ib, ia = pair(high_quads, low_quads, "gx")
    shapes = coefficient_shapes(*WINDOWS, *WHOLES) + [weights, jax.ShapeDtypeStruct((6, 256, 256), BF16)]
    c1, d1, c2, d2, c3o, d3o, c3, _, c4, d4, c5, d5, c6, _, halving, doubling = call(
        geometry_kernel, tuple(shapes), []
    )(low_quads)

    def quad_ends(low):
        return jnp.concatenate([part[:, low : low + 16] for part in (ib, low_quads, high_quads, ia)], axis=0)

    jb, ja = pair(quad_ends(16), quad_ends(0), "gy")
    qf, ku, kd = call(pack_quads_kernel, (struct(16, 64, 128), struct(8, 64, 128), struct(8, 64, 128)), [])(
        ib, ia, low_quads, high_quads, jb, ja
    )
    kb, ka = pair(ku, kd, "gz", True)
    s1, s2, s3 = L1.shape(), L2.shape(), L3_OWN.shape()
    v1, gr1, gb1, v2, gr2, gb2, message = call(
        middle_kernel,
        tuple(struct(*s) for s in (s1, s1, s1, s2, s2, s2, (64, 5, 1, 128))),
        [s1, s1, (28, 32, 128), (28, 32, 128), s2, s2, (12, 16, 128), (12, 16, 128)]
        + [s3, s3, s3, s3, s3, (4, 8, 128), (4, 8, 128), (8, 16, 128)],
    )(qf, kb, ka, c1, d1, c2, d2, c3o, d3o, halving)

    tiles = lax.all_to_all(message, ("gy", "gz"), 0, 0)
    message, near = call(
        plane_kernel, (struct(8, 56, 128), struct(8, 24, 128)), [(64, 128), (32, 128), (9, 8, 128)]
    )(tiles)
    tiles = lax.all_to_all(message, "gx", 0, 0)
    s3, s4, s5, s6 = L3.shape(), L4.shape(), L5.shape(), L6.shape()
    return tuple(
        call(
            coarse_kernel,
            (struct(64, 64, 64), struct(64, 64, 64)),
            [s4, s4, s4, s4, s4, (16, 16, 128), (16, 16, 128)]
            + [s5, s5, s5, s5, s5, (8, 8, 128), (8, 8, 128)]
            + [s6, s6, s6, s6, (40, 48, 128)]
            + [s3, s3, s3, s3, s3, s2, s2, s1, s1, fine, fine, fine]
            + [(42, 40, 128), (42, 40, 128), (42, 40, 128), (40, 64, 128), (16, 80, 128), (64, 64, 64), (64, 64, 64)],
            out_space=pl.ANY,
            semaphores=16,
        )(tiles, near, v2, gr2, gb2, v1, gr1, gb1, v0, gr0, gb0, c0, d0, c1, c2, c3, c4, d4, c5, d5, c6, halving, doubling)
    )


def solution(mesh):
    return jax.shard_map(
        per_device,
        mesh=mesh,
        in_specs=(P("gx", "gy", "gz"), P("gx", "gy", "gz")),
        out_specs=(P("gx", "gy", "gz"), P("gx", "gy", "gz")),
        check_vma=False,
    )
```

time: 184 us -> 120 us (0.65)
  Pallas kernels: 69.8 us -> 23.5 us
  starting transfers between devices: 37.5 us -> 29.9 us
  blocking collectives: 46.1 us -> 41.5 us
  waiting for transfers between devices: 25.6 us -> 21.1 us
    pallas_call x7 -> x10, Pallas kernels: 69.8 us -> 23.5 us  [run(): pl.pallas_call(kernel, out_shape=outs, in_specs=[space] * len(args), out_...]
    ppermute x12, starting transfers between devices: 37.5 us -> 29.9 us  [the longest x6 23.1 us: pair(): before = lax.ppermute(to_next, axis, up)]
    all_to_all x1, blocking collectives: 28.2 us -> 21.4 us  [per_device(): tiles = lax.all_to_all(message, ('gy', 'gz'), 0, 0)]
    ppermute x12, waiting for transfers between devices: 25.6 us -> 21.1 us  [the longest x6 17.1 us: pair(): after = lax.ppermute(to_before, axis, down)]
    all_to_all x1, blocking collectives: 17.8 us -> 20.1 us  [per_device(): tiles = lax.all_to_all(message, 'gx', 0, 0)]
  transfers between devices with their start and end apart: 12 -> 12, of which waited for: 10 -> 8; matrix products, arithmetic and copies ran while one was open for 0% -> 1% of each run, Pallas kernels for 1% -> 3%
where the time goes in v2:
time: 120 us
  blocking collectives  41.5 us (35%)
  starting transfers between devices  29.9 us (25%)
  Pallas kernels  23.5 us (20%)
  waiting for transfers between devices  21.1 us (18%)
  other arithmetic  1.65 us (1%)
    pallas_call x10, Pallas kernels, run(): pl.pallas_call(kernel, out_shape=outs, in_specs=[space] * len(args), out_...  23.5 us
    ppermute x6, starting transfers between devices, pair(): before = lax.ppermute(to_next, axis, up)  23.1 us
    all_to_all x1, blocking collectives, per_device(): tiles = lax.all_to_all(message, ('gy', 'gz'), 0, 0)  21.4 us
    all_to_all x1, blocking collectives, per_device(): tiles = lax.all_to_all(message, 'gx', 0, 0)  20.1 us
    ppermute x6, waiting for transfers between devices, pair(): after = lax.ppermute(to_before, axis, down)  17.1 us
    ppermute x6, starting transfers between devices, pair(): after = lax.ppermute(to_before, axis, down)  6.79 us
    ppermute x6, waiting for transfers between devices, pair(): before = lax.ppermute(to_next, axis, up)  3.96 us
  transfers between devices with their start and end apart: 12, of which 8 were waited for; matrix products, arithmetic and copies ran while one was open for 1% of the time, Pallas kernels for 3%

profile of v2, /device:TPU:1, one launch (start us, length us, event | category | flops | bytes accessed | tf_op | source)
XLA Modules:
  0.0 119.8 jit_solution(949469664297209075)
XLA Ops:
  0.7 1.4 %slice_select_fusion = (f32[3,64,64]{2,1,0:T(8,128)S(1)}, f32[3,64,64]{2,1,0:T(8,128)S(1)}, f32[3,64,64]{2,1,0:T(8,128)S(1)}, f32[3,64,64]{2,1,0:T(8,128)S(1)}, ...) fusion(f32[64,64,64]{2,1,0:T(8,128)} %guess.1, pred[64,64]{1,0:T(8,128)(4,1)S(1)} %and_compare_fusion, ...), kind=kLoop, calls=%fused_computation.4 | loop fusion | flops 73728 | bytes 692224 | tf_op jit(solution)/shard_map/jit(_where)/select_n | solution.py:928
  2.2 1.4 %collective-permute-start.1 = (f32[4,64,128]{2,1,0:T(8,128)S(1)}, f32[4,64,128]{2,1,0:T(8,128)S(1)}, u32[]{:S(2)}, u32[]{:S(2)}) collective-permute-start(f32[4,64,128]{2,1,0:T(8,128)S(1)} %maximum_maximum_fusion.1), channel_id=1, source_target_pairs={{64,0},{128,64},{192,128},{256,192},{320,256},{384,320},{448,384},... | collective-permute-start | bytes 393224 | tf_op jit(solution)/shard_map/ppermute | solution.py:917
  3.8 5.5 %collective-permute-start = (f32[4,64,128]{2,1,0:T(8,128)S(1)}, f32[4,64,128]{2,1,0:T(8,128)S(1)}, u32[]{:S(2)}, u32[]{:S(2)}) collective-permute-start(f32[4,64,128]{2,1,0:T(8,128)S(1)} %maximum_maximum_fusion), channel_id=1, source_target_pairs={{0,64},{64,128},{128,192},{192,256},{256,320},{320,384},{384,448},... | collective-permute-start | bytes 393224 | tf_op jit(solution)/shard_map/ppermute | solution.py:918
  9.2 1.1 fusion
  10.4 0.8 collective-permute-done.ib
  11.3 3.4 %collective-permute-start.2 = (f32[248,128]{1,0:T(8,128)S(1)}, f32[248,128]{1,0:T(8,128)S(1)}, u32[]{:S(2)}, u32[]{:S(2)}) collective-permute-start(f32[248,128]{1,0:T(8,128)S(1)} %get-tuple-element.49), channel_id=1, source_target_pairs={{0,8},{8,16},{16,24},{24,32},{32,40},{40,48},{48,56},{1,9},{9,17},... | collective-permute-start | bytes 380936 | tf_op jit(solution)/shard_map/ppermute | solution.py:918
  14.8 1.3 %collective-permute-start.3 = (f32[248,128]{1,0:T(8,128)S(1)}, f32[248,128]{1,0:T(8,128)S(1)}, u32[]{:S(2)}, u32[]{:S(2)}) collective-permute-start(f32[248,128]{1,0:T(8,128)S(1)} %get-tuple-element.50), channel_id=1, source_target_pairs={{8,0},{16,8},{24,16},{32,24},{40,32},{48,40},{56,48},{9,1},{17,9},... | collective-permute-start | bytes 380936 | tf_op jit(solution)/shard_map/ppermute | solution.py:917
  16.1 1.0 shard_map.41
  17.1 3.4 %collective-permute-done.3.ja = f32[248,128]{1,0:T(8,128)S(1)} collective-permute-done((f32[248,128]{1,0:T(8,128)S(1)}, f32[248,128]{1,0:T(8,128)S(1)}, u32[]{:S(2)}, u32[]{:S(2)}) %collective-permute-start.3) | collective-permute-done | bytes 127008 | tf_op jit(solution)/shard_map/ppermute | solution.py:917
  20.4 1.0 shard_map.43
  21.4 4.1 %collective-permute-start.4 = (f32[5,80,128]{2,1,0:T(8,128)S(1)}, f32[5,80,128]{2,1,0:T(8,128)S(1)}, u32[]{:S(2)}, u32[]{:S(2)}) collective-permute-start(f32[5,80,128]{2,1,0:T(8,128)S(1)} %get-tuple-element.56), channel_id=1, source_target_pairs={{0,1},{1,2},{2,3},{3,4},{4,5},{5,6},{6,7},{7,0},{8,9},{9,10},{10,1... | collective-permute-start | bytes 614408 | tf_op jit(solution)/shard_map/ppermute | solution.py:918
  25.5 1.5 %collective-permute-start.5 = (f32[5,80,128]{2,1,0:T(8,128)S(1)}, f32[5,80,128]{2,1,0:T(8,128)S(1)}, u32[]{:S(2)}, u32[]{:S(2)}) collective-permute-start(f32[5,80,128]{2,1,0:T(8,128)S(1)} %get-tuple-element.57), channel_id=1, source_target_pairs={{1,0},{2,1},{3,2},{4,3},{5,4},{6,5},{7,6},{0,7},{9,8},{10,9},{11,1... | collective-permute-start | bytes 614408 | tf_op jit(solution)/shard_map/ppermute | solution.py:917
  27.0 1.7 %shard_map.44 = (f32[42,80,128]{2,1,0:T(8,128)S(1)}, f32[42,80,128]{2,1,0:T(8,128)S(1)}, f32[42,80,128]{2,1,0:T(8,128)S(1)}, f32[4,80,128]{2,1,0:T(8,128)S(1)}, ...) custom-call(f32[40,80,128]{2,1,0:T(8,128)S(1)} %get-tuple-element.51.xf, f32[24,80,128]{2,1,0:T(8,128)S(1)} %get-tuple-element.52.yf), custom_call_target="tpu_custom_call" | custom-call | flops 2000000 | bytes 1000000 | tf_op jit(solution)/shard_map/pallas_call | solution.py:901
  28.7 2.3 %collective-permute-done.5.ka = f32[5,80,128]{2,1,0:T(8,128)S(1)} collective-permute-done((f32[5,80,128]{2,1,0:T(8,128)S(1)}, f32[5,80,128]{2,1,0:T(8,128)S(1)}, u32[]{:S(2)}, u32[]{:S(2)}) %collective-permute-start.5) | collective-permute-done | bytes 204832 | tf_op jit(solution)/shard_map/ppermute | solution.py:917
  31.0 5.1 %shard_map.45 = (f32[42,80,128]{2,1,0:T(8,128)S(1)}, f32[42,80,128]{2,1,0:T(8,128)S(1)}, f32[42,80,128]{2,1,0:T(8,128)S(1)}, f32[4,32,128]{2,1,0:T(8,128)S(1)}, f32[4,32,128]{2,1,0:T(8,128)S(1)}) custom-call(f32[42,80,128]{2,1,0:T(8,128)S(1)} %get-tuple-element.53.black0, f32[42,80,128]{2,1,0:T(8,128)S(1)} %get-tuple-element.54.g_red0, ...), custom_call_target="tpu_custom_call" | custom-call | flops 2000000 | bytes 1000000 | tf_op jit(solution)/shard_map/pallas_call | solution.py:901
  36.1 4.1 %collective-permute-start.6 = (f32[4,32,128]{2,1,0:T(8,128)S(1)}, f32[4,32,128]{2,1,0:T(8,128)S(1)}, u32[]{:S(2)}, u32[]{:S(2)}) collective-permute-start(f32[4,32,128]{2,1,0:T(8,128)S(1)} %get-tuple-element.61.high_quads), channel_id=1, source_target_pairs={{0,64},{64,128},{128,192},{192,256},{256,320},{320,384},{384,448},... | collective-permute-start | bytes 196616 | tf_op jit(solution)/shard_map/ppermute | solution.py:918
  40.3 1.3 %collective-permute-start.7 = (f32[4,32,128]{2,1,0:T(8,128)S(1)}, f32[4,32,128]{2,1,0:T(8,128)S(1)}, u32[]{:S(2)}, u32[]{:S(2)}) collective-permute-start(f32[4,32,128]{2,1,0:T(8,128)S(1)} %get-tuple-element.62.low_quads.after), channel_id=1, source_target_pairs={{64,0},{128,64},{192,128},{256,192},{320,256},{384,320},{448,384},... | collective-permute-start | bytes 196616 | tf_op jit(solution)/shard_map/ppermute | solution.py:917
  41.6 4.0 %collective-permute-done.7.ia = f32[4,32,128]{2,1,0:T(8,128)S(1)} collective-permute-done((f32[4,32,128]{2,1,0:T(8,128)S(1)}, f32[4,32,128]{2,1,0:T(8,128)S(1)}, u32[]{:S(2)}, u32[]{:S(2)}) %collective-permute-start.7) | collective-permute-done | bytes 65568 | tf_op jit(solution)/shard_map/ppermute | solution.py:917
  45.6 3.2 %collective-permute-start.8 = (f32[16,16,128]{2,1,0:T(8,128)S(1)}, f32[16,16,128]{2,1,0:T(8,128)S(1)}, u32[]{:S(2)}, u32[]{:S(2)}) collective-permute-start(f32[16,16,128]{2,1,0:T(8,128)S(1)} %pad_maximum_fusion), channel_id=1, source_target_pairs={{0,8},{8,16},{16,24},{24,32},{32,40},{40,48},{48,56},{1,9},{9,17},... | collective-permute-start | bytes 393224 | tf_op jit(solution)/shard_map/ppermute | solution.py:918
  48.9 1.3 %collective-permute-start.9 = (f32[16,16,128]{2,1,0:T(8,128)S(1)}, f32[16,16,128]{2,1,0:T(8,128)S(1)}, u32[]{:S(2)}, u32[]{:S(2)}) collective-permute-start(f32[16,16,128]{2,1,0:T(8,128)S(1)} %pad_maximum_fusion.1), channel_id=1, source_target_pairs={{8,0},{16,8},{24,16},{32,24},{40,32},{48,40},{56,48},{9,1},{17,9},... | collective-permute-start | bytes 393224 | tf_op jit(solution)/shard_map/ppermute | solution.py:917
  50.2 0.6 collective-permute-done.8.jb
  50.8 4.8 %collective-permute-done.9.ja = f32[16,16,128]{2,1,0:T(8,128)S(1)} collective-permute-done((f32[16,16,128]{2,1,0:T(8,128)S(1)}, f32[16,16,128]{2,1,0:T(8,128)S(1)}, u32[]{:S(2)}, u32[]{:S(2)}) %collective-permute-start.9) | collective-permute-done | bytes 131104 | tf_op jit(solution)/shard_map/ppermute | solution.py:917
  55.6 0.9 shard_map.46
  56.5 2.9 %collective-permute-start.10 = (f32[8,64,128]{2,1,0:T(8,128)S(1)}, f32[8,64,128]{2,1,0:T(8,128)S(1)}, u32[]{:S(2)}, u32[]{:S(2)}) collective-permute-start(f32[8,64,128]{2,1,0:T(8,128)S(1)} %get-tuple-element.64), channel_id=1, source_target_pairs={{0,1},{1,2},{2,3},{3,4},{4,5},{5,6},{6,7},{7,0},{8,9},{9,10},{10,1... | collective-permute-start | bytes 786440 | tf_op jit(solution)/shard_map/ppermute | solution.py:918
  59.3 0.8 shard_map.47
  60.1 2.6 %collective-permute-done.10.kb = f32[8,64,128]{2,1,0:T(8,128)S(1)} collective-permute-done((f32[8,64,128]{2,1,0:T(8,128)S(1)}, f32[8,64,128]{2,1,0:T(8,128)S(1)}, u32[]{:S(2)}, u32[]{:S(2)}) %collective-permute-start.10) | collective-permute-done | bytes 262176 | tf_op jit(solution)/shard_map/ppermute | solution.py:918
  62.6 2.6 %collective-permute-done.11.ka = f32[8,64,128]{2,1,0:T(8,128)S(1)} collective-permute-done((f32[8,64,128]{2,1,0:T(8,128)S(1)}, f32[8,64,128]{2,1,0:T(8,128)S(1)}, u32[]{:S(2)}, u32[]{:S(2)}) %collective-permute-start.11) | collective-permute-done | bytes 262176 | tf_op jit(solution)/shard_map/ppermute | solution.py:917
  65.2 3.1 %shard_map.48 = (f32[32,64,128]{2,1,0:T(8,128)S(1)}, f32[32,64,128]{2,1,0:T(8,128)S(1)}, f32[32,64,128]{2,1,0:T(8,128)S(1)}, f32[16,32,128]{2,1,0:T(8,128)S(1)},...) custom-call(f32[16,64,128]{2,1,0:T(8,128)S(1)} %get-tuple-element.63.qf, ...), custom_call_target="tpu_custom_call" | custom-call | flops 2000000 | bytes 1000000 | tf_op jit(solution)/shard_map/pallas_call | solution.py:901
  68.4 21.4 %all_to_all.10.tiles = f32[64,5,1,128]{3,2,1,0:T(1,128)S(1)} all-to-all(f32[64,5,1,128]{3,2,1,0:T(1,128)S(1)} %get-tuple-element.73), channel_id=1, replica_groups=mesh['gx'=8,'gy'=8,'gz'=8] {'gy','gz'}, dimensions={0} | all-to-all | bytes 327680 | tf_op jit(solution)/shard_map/all_to_all | solution.py:985
  89.8 0.4 shard_map.49
  90.2 20.1 %all_to_all.11.tiles = f32[8,56,128]{2,1,0:T(8,128)S(1)} all-to-all(f32[8,56,128]{2,1,0:T(8,128)S(1)} %get-tuple-element.74), channel_id=1, replica_groups=mesh['gx'=8,'gy'=8,'gz'=8] {'gx'}, dimensions={0} | all-to-all | bytes 458752 | tf_op jit(solution)/shard_map/all_to_all | solution.py:989
  110.2 9.4 %shard_map.50 = (f32[64,64,64]{2,1,0:T(8,128)}, f32[64,64,64]{2,1,0:T(8,128)}) custom-call(f32[8,56,128]{2,1,0:T(8,128)S(1)} %all_to_all.11.tiles, f32[8,24,128]{2,1,0:T(8,128)S(1)} %get-tuple-element.75.near, f32[16,32,128]{2,1,0:T(8,128)S(1)} %get-tuple-element.76.v2, f32[16,32,128]{2,1,0:T(8,128)S(1)} %get-tuple-element.77.gr2, ...), custom_call_target="tpu_custom_call" | custom-call | flops 2000000 | bytes 1000000 | tf_op jit(solution)/shard_map/pallas_call | solution.py:901
  (21 shorter events, 0.5 us)
Async XLA Ops:
  0.6 8.6 %copy-start = (f32[64,64,64]{2,1,0:T(8,128)S(1)}, f32[64,64,64]{2,1,0:T(8,128)}, u32[]{:S(2)}) copy-start(f32[64,64,64]{2,1,0:T(8,128)} %guess.1) | copy-start | bytes 3145732
  2.1 14.0 %copy-start.1 = (f32[64,64,64]{2,1,0:T(8,128)S(1)}, f32[64,64,64]{2,1,0:T(8,128)}, u32[]{:S(2)}) copy-start(f32[64,64,64]{2,1,0:T(8,128)} %source.1) | copy-start | bytes 3145732
  2.2 8.1 %collective-permute-start.1 = (f32[4,64,128]{2,1,0:T(8,128)S(1)}, f32[4,64,128]{2,1,0:T(8,128)S(1)}, u32[]{:S(2)}, u32[]{:S(2)}) collective-permute-start(f32[4,64,128]{2,1,0:T(8,128)S(1)} %maximum_maximum_fusion.1), channel_id=1, source_target_pairs={{64,0},{128,64},{192,128},{256,192},{320,256},{384,320},{448,384},... | collective-permute-start | bytes 393224 | tf_op jit(solution)/shard_map/ppermute | solution.py:917
  3.8 7.4 %collective-permute-start = (f32[4,64,128]{2,1,0:T(8,128)S(1)}, f32[4,64,128]{2,1,0:T(8,128)S(1)}, u32[]{:S(2)}, u32[]{:S(2)}) collective-permute-start(f32[4,64,128]{2,1,0:T(8,128)S(1)} %maximum_maximum_fusion), channel_id=1, source_target_pairs={{0,64},{64,128},{128,192},{192,256},{256,320},{320,384},{384,448},... | collective-permute-start | bytes 393224 | tf_op jit(solution)/shard_map/ppermute | solution.py:918
  11.3 5.7 %collective-permute-start.2 = (f32[248,128]{1,0:T(8,128)S(1)}, f32[248,128]{1,0:T(8,128)S(1)}, u32[]{:S(2)}, u32[]{:S(2)}) collective-permute-start(f32[248,128]{1,0:T(8,128)S(1)} %get-tuple-element.49), channel_id=1, source_target_pairs={{0,8},{8,16},{16,24},{24,32},{32,40},{40,48},{48,56},{1,9},{9,17},... | collective-permute-start | bytes 380936 | tf_op jit(solution)/shard_map/ppermute | solution.py:918
  14.8 5.7 %collective-permute-start.3 = (f32[248,128]{1,0:T(8,128)S(1)}, f32[248,128]{1,0:T(8,128)S(1)}, u32[]{:S(2)}, u32[]{:S(2)}) collective-permute-start(f32[248,128]{1,0:T(8,128)S(1)} %get-tuple-element.50), channel_id=1, source_target_pairs={{8,0},{16,8},{24,16},{32,24},{40,32},{48,40},{56,48},{9,1},{17,9},... | collective-permute-start | bytes 380936 | tf_op jit(solution)/shard_map/ppermute | solution.py:917
  21.4 7.3 %collective-permute-start.4 = (f32[5,80,128]{2,1,0:T(8,128)S(1)}, f32[5,80,128]{2,1,0:T(8,128)S(1)}, u32[]{:S(2)}, u32[]{:S(2)}) collective-permute-start(f32[5,80,128]{2,1,0:T(8,128)S(1)} %get-tuple-element.56), channel_id=1, source_target_pairs={{0,1},{1,2},{2,3},{3,4},{4,5},{5,6},{6,7},{7,0},{8,9},{9,10},{10,1... | collective-permute-start | bytes 614408 | tf_op jit(solution)/shard_map/ppermute | solution.py:918
  25.5 5.5 %collective-permute-start.5 = (f32[5,80,128]{2,1,0:T(8,128)S(1)}, f32[5,80,128]{2,1,0:T(8,128)S(1)}, u32[]{:S(2)}, u32[]{:S(2)}) collective-permute-start(f32[5,80,128]{2,1,0:T(8,128)S(1)} %get-tuple-element.57), channel_id=1, source_target_pairs={{1,0},{2,1},{3,2},{4,3},{5,4},{6,5},{7,6},{0,7},{9,8},{10,9},{11,1... | collective-permute-start | bytes 614408 | tf_op jit(solution)/shard_map/ppermute | solution.py:917
  36.1 5.4 %collective-permute-start.6 = (f32[4,32,128]{2,1,0:T(8,128)S(1)}, f32[4,32,128]{2,1,0:T(8,128)S(1)}, u32[]{:S(2)}, u32[]{:S(2)}) collective-permute-start(f32[4,32,128]{2,1,0:T(8,128)S(1)} %get-tuple-element.61.high_quads), channel_id=1, source_target_pairs={{0,64},{64,128},{128,192},{192,256},{256,320},{320,384},{384,448},... | collective-permute-start | bytes 196616 | tf_op jit(solution)/shard_map/ppermute | solution.py:918
  40.3 5.4 %collective-permute-start.7 = (f32[4,32,128]{2,1,0:T(8,128)S(1)}, f32[4,32,128]{2,1,0:T(8,128)S(1)}, u32[]{:S(2)}, u32[]{:S(2)}) collective-permute-start(f32[4,32,128]{2,1,0:T(8,128)S(1)} %get-tuple-element.62.low_quads.after), channel_id=1, source_target_pairs={{64,0},{128,64},{192,128},{256,192},{320,256},{384,320},{448,384},... | collective-permute-start | bytes 196616 | tf_op jit(solution)/shard_map/ppermute | solution.py:917
  45.6 5.1 %collective-permute-start.8 = (f32[16,16,128]{2,1,0:T(8,128)S(1)}, f32[16,16,128]{2,1,0:T(8,128)S(1)}, u32[]{:S(2)}, u32[]{:S(2)}) collective-permute-start(f32[16,16,128]{2,1,0:T(8,128)S(1)} %pad_maximum_fusion), channel_id=1, source_target_pairs={{0,8},{8,16},{16,24},{24,32},{32,40},{40,48},{48,56},{1,9},{9,17},... | collective-permute-start | bytes 393224 | tf_op jit(solution)/shard_map/ppermute | solution.py:918
  48.9 6.7 %collective-permute-start.9 = (f32[16,16,128]{2,1,0:T(8,128)S(1)}, f32[16,16,128]{2,1,0:T(8,128)S(1)}, u32[]{:S(2)}, u32[]{:S(2)}) collective-permute-start(f32[16,16,128]{2,1,0:T(8,128)S(1)} %pad_maximum_fusion.1), channel_id=1, source_target_pairs={{8,0},{16,8},{24,16},{32,24},{40,32},{48,40},{56,48},{9,1},{17,9},... | collective-permute-start | bytes 393224 | tf_op jit(solution)/shard_map/ppermute | solution.py:917
  56.5 6.2 %collective-permute-start.10 = (f32[8,64,128]{2,1,0:T(8,128)S(1)}, f32[8,64,128]{2,1,0:T(8,128)S(1)}, u32[]{:S(2)}, u32[]{:S(2)}) collective-permute-start(f32[8,64,128]{2,1,0:T(8,128)S(1)} %get-tuple-element.64), channel_id=1, source_target_pairs={{0,1},{1,2},{2,3},{3,4},{4,5},{5,6},{6,7},{7,0},{8,9},{9,10},{10,1... | collective-permute-start | bytes 786440 | tf_op jit(solution)/shard_map/ppermute | solution.py:918
  59.3 5.9 %collective-permute-start.11 = (f32[8,64,128]{2,1,0:T(8,128)S(1)}, f32[8,64,128]{2,1,0:T(8,128)S(1)}, u32[]{:S(2)}, u32[]{:S(2)}) collective-permute-start(f32[8,64,128]{2,1,0:T(8,128)S(1)} %get-tuple-element.65), channel_id=1, source_target_pairs={{1,0},{2,1},{3,2},{4,3},{5,4},{6,5},{7,6},{0,7},{9,8},{10,9},{11,1... | collective-permute-start | bytes 786440 | tf_op jit(solution)/shard_map/ppermute | solution.py:917
